TPU v7x, 32 devices: a 4x4x1 block of a 4x4x8 slice. The times are simulated.
32 devices in a mesh: dp: 1 (over z), tp: 32 (over y, x, core).
Axes of the slice: x: 4, y: 4, z: 1, core: 2. Of those that a mesh axis runs over, the one named last changes fastest.
The devices are a block of a 4x4x8 slice.
Arguments:
- hidden: bfloat16 [512, 4096], P('dp')
- w_gate: bfloat16 [4096, 11008], P(None, 'tp')
- w_up: bfloat16 [4096, 11008], P(None, 'tp')
- w_down: bfloat16 [11008, 4096], P('tp')
- norm_gain: float32 [4096], replicated
- w_vocab: bfloat16 [4096, 32000], P(None, 'tp')
- temperature: float32 [512], P('dp')
- target: int32 [512], P('dp')
Outputs:
- output 1: float32 [512], P('dp')
- output 2: float32 [512], P('dp')
- output 3: float32 [512], P('dp')
- output 4: bfloat16 [512, 32000], P('dp')
All inputs are finite; a program needn't handle non-finite values.
Results may differ from a plain program's by a relative error of at most 0.00463344.
Values are sent between devices in bfloat16 or wider.
A program may use at most 768 MiB of HBM per device.

v0:
```python
import jax
import jax.numpy as jnp
from jax import lax
from jax.sharding import PartitionSpec as P

NORM_EPS = 1e-6


def solution(mesh):
    def device_step(hidden, w_gate, w_up, w_down, norm_gain, w_vocab, value_a11, target):
        gate_pre = jnp.dot(hidden, w_gate, preferred_element_type=jnp.float32)
        up_pre = jnp.dot(hidden, w_up, preferred_element_type=jnp.float32)
        hidden_act = (jax.nn.silu(gate_pre) * up_pre).astype(jnp.bfloat16)
        part_sum = jnp.dot(hidden_act, w_down, preferred_element_type=jnp.float32).astype(jnp.bfloat16)
        mlp_out = lax.psum(part_sum, "tp")
        residual = hidden.astype(jnp.float32) + mlp_out.astype(jnp.float32)
        inv_rms = lax.rsqrt(jnp.mean(residual * residual, axis=-1, keepdims=True) + NORM_EPS)
        normed = (norm_gain * residual * inv_rms).astype(jnp.bfloat16)
        logits = jnp.dot(normed, w_vocab, preferred_element_type=jnp.float32) / value_a11[:, None]
        vocab_local = logits.shape[1]
        row_max = lax.pmax(jnp.max(logits, axis=-1), "tp")
        shifted = jnp.exp(logits - row_max[:, None])
        local_ids = target - lax.axis_index("tp") * vocab_local
        col_ids = jnp.arange(vocab_local, dtype=jnp.int32)
        target_hit = jnp.where(col_ids[None, :] == local_ids[:, None], logits, 0.0)
        local_stats = jnp.stack(
            [jnp.sum(shifted, axis=-1), jnp.sum(shifted * logits, axis=-1), jnp.sum(target_hit, axis=-1)], axis=0)
        row_stats = lax.psum(local_stats, "tp")
        sum_exp = row_stats[0]
        weighted_sum = row_stats[1]
        target_logit = row_stats[2]
        log_norm = row_max + jnp.log(sum_exp)
        entropy = log_norm - weighted_sum / sum_exp
        target_logp = target_logit - log_norm
        local_probs = (logits - log_norm[:, None]).astype(jnp.bfloat16)
        log_probs = lax.all_gather(local_probs, "tp", axis=1, tiled=True)
        return log_norm, entropy, target_logp, log_probs

    return jax.shard_map(
        device_step,
        mesh=mesh,
        in_specs=(P("dp", None), P(None, "tp"), P(None, "tp"), P("tp", None), P(None),
                  P(None, "tp"), P("dp"), P("dp")),
        out_specs=(P("dp"), P("dp"), P("dp"), P("dp", None)),
        check_vma=False,
    )
```

profile of v0, /device:TPU:97, one launch (start us, length us, event | category | flops | bytes accessed | tf_op | source)
XLA Modules:
  0.0 384.1 jit_solution(7983973243219671025)
XLA Ops:
  7.2 0.0 copy-start
  7.2 0.1 all-reduce.2.cloned.1.call-start
  7.3 4.9 %fusion.10 = f32[512,344]{0,1:T(8,128)S(1)} fusion(bf16[512,4096]{1,0:T(8,128)(2,1)} %param.8, bf16[4096,344]{0,1:T(8,128)(2,1)} %param.9), kind=kOutput, calls=%fused_computation.25 | convolution fusion | flops 1442840576 | bytes 7716864 | tf_op jit(solution)/shard_map/dot_general | solution.py:11
  12.1 0.0 copy-done
  12.1 9.1 %convolution_convert_fusion = bf16[512,4096]{1,0:T(8,128)(2,1)} fusion(bf16[344,4096]{1,0:T(8,128)(2,1)S(1)} %copy-done, bf16[512,4096]{1,0:T(8,128)(2,1)} %param.8, bf16[4096,344]{0,1:T(8,128)(2,1)} %param.10, f32[512,344]{0,1:T(8,128)S(1)} %fusion.10), kind=kOutput, calls=%fused_computation.3 | convolution fusion | flops 2888835072 | bytes 14729216 | tf_op jit(solution)/shard_map/dot_general | solution.py:14
  21.3 0.0 copy-start.5
  21.3 0.0 copy-start.6
  21.3 0.1 all-reduce.2.cloned.1.call-update
  21.3 0.1 all-gather.2.cloned.1.call-start
  21.4 0.5 copy-done.5
  22.0 0.0 copy-start.7
  22.0 104.7 %all-reduce.2.cloned.1.call-done = bf16[512,4096]{1,0:T(8,128)(2,1)} async-done(((bf16[512,4096]{1,0:T(8,128)(2,1)}), bf16[512,4096]{1,0:T(8,128)(2,1)}) %all-reduce.2.cloned.1.call-update) | async-done | bytes 4194320 | tf_op jit(solution)/shard_map/psum | solution.py:15
  126.6 0.0 copy-start.2
  126.6 0.0 copy-start.3
  126.6 5.0 %multiply_reduce_fusion = f32[512]{0:T(512)S(1)} fusion(bf16[512,4096]{1,0:T(8,128)(2,1)} %all-reduce.2.cloned.1.call-done, bf16[512,4096]{1,0:T(8,128)(2,1)} %param.8), kind=kLoop, calls=%fused_computation.1 | loop fusion | flops 10485248 | bytes 8390656 | tf_op jit(solution)/shard_map/reduce_sum | solution.py:17
  131.7 0.0 copy-done.6
  131.7 0.0 copy-done.7
  131.7 0.0 copy-done.2
  131.7 0.8 copy-done.3
  132.5 7.7 %fusion.9 = (f32[512]{0:T(512)S(1)}, f32[512,1000]{0,1:T(8,128)S(1)}) fusion(f32[512]{0:T(512)S(1)} %copy-done.7, bf16[4096,1000]{0,1:T(8,128)(2,1)} %param.13, bf16[512,4096]{1,0:T(8,128)(2,1)S(1)} %copy-done.3, bf16[512,4096]{1,0:T(8,128)(2,1)S(1)} %copy-done.2, f32[512]{0:T(512)S(1)} %add_rsqrt_fusion, f32[4096]{0:T(1024)S(1)} %copy-done.6), kind=kOutput, calls=%fused_computation.24 | convolution fusion | flops 4207910400 | bytes 18651136 | tf_op jit(solution)/shard_map/dot_general | solution.py:19
  140.3 45.7 %pmax.7 = f32[512]{0:T(512)S(1)} all-reduce(f32[512]{0:T(512)S(1)} %get-tuple-element.16), channel_id=1, replica_groups=mesh['dp'=1,'tp'=32] {'tp'}, use_global_device_ids=true, to_apply=%region_3.4 | all-reduce | flops 512 | bytes 4096 | tf_op jit(solution)/shard_map/pmax | solution.py:21
  186.0 0.7 fusion.3
  186.7 43.6 %psum.15 = f32[3,512]{1,0:T(4,128)S(1)} all-reduce(f32[3,512]{1,0:T(4,128)S(1)} %pad_maximum_fusion), channel_id=1, replica_groups=mesh['dp'=1,'tp'=32] {'tp'}, use_global_device_ids=true, to_apply=%region_7.8 | all-reduce | flops 1536 | bytes 12288 | tf_op jit(solution)/shard_map/psum | solution.py:28
  230.2 0.6 fusion.8
  230.8 0.0 copy-start.4
  230.8 1.2 subtract_convert_fusion
  232.1 0.1 all-gather.2.cloned.1.call-update
  232.1 0.6 sub.32
  232.7 104.1 %all-gather.2.cloned.1.call-done = bf16[512,32000]{0,1:T(8,128)(2,1)} async-done(((bf16[512,1000]{0,1:T(8,128)(2,1)}), bf16[512,32000]{0,1:T(8,128)(2,1)}) %all-gather.2.cloned.1.call-update) | async-done | bytes 32768016 | tf_op jit(solution)/shard_map/all_gather | solution.py:36
  336.8 0.0 copy-start.1
  336.8 40.4 %copy.12 = bf16[512,32000]{1,0:T(8,128)(2,1)} copy(bf16[512,32000]{0,1:T(8,128)(2,1)} %all-gather.2.cloned.1.call-done) | data formatting | bytes 65536000
  377.3 0.0 copy-done.4
  377.3 0.0 copy-done.1
  (4 shorter events, 0.0 us)
Async XLA Ops:
  7.2 5.0 %copy-start = (bf16[344,4096]{1,0:T(8,128)(2,1)S(1)}, bf16[344,4096]{1,0:T(8,128)(2,1)}, u32[]{:S(2)}) copy-start(bf16[344,4096]{1,0:T(8,128)(2,1)} %param.11) | copy-start | bytes 8454148
  7.2 119.4 %all-reduce.2.cloned.1.call-start = ((), (), s32[]{:S(2)}) async-start(), calls=%async_computation | async-start | bytes 8388608 | tf_op jit(solution)/shard_map/psum | solution.py:15
  21.3 0.7 copy-start.5
  21.3 110.4 %copy-start.6 = (f32[4096]{0:T(1024)S(1)}, f32[4096]{0:T(1024)}, u32[]{:S(2)}) copy-start(f32[4096]{0:T(1024)} %param.12) | copy-start | bytes 49156
  21.3 315.5 %all-gather.2.cloned.1.call-start = ((), (), s32[]{:S(2)}) async-start(), calls=%async_computation.1 | async-start | bytes 33792000 | tf_op jit(solution)/shard_map/all_gather | solution.py:36
  22.0 109.7 %copy-start.7 = (f32[512]{0:T(512)S(1)}, f32[512]{0:T(512)}, u32[]{:S(2)}) copy-start(f32[512]{0:T(512)} %param.14) | copy-start | bytes 6148
  126.6 5.1 %copy-start.2 = (bf16[512,4096]{1,0:T(8,128)(2,1)S(1)}, bf16[512,4096]{1,0:T(8,128)(2,1)}, u32[]{:S(2)}) copy-start(bf16[512,4096]{1,0:T(8,128)(2,1)} %param.8) | copy-start | bytes 12582916
  126.6 5.9 %copy-start.3 = (bf16[512,4096]{1,0:T(8,128)(2,1)S(1)}, bf16[512,4096]{1,0:T(8,128)(2,1)}, u32[]{:S(2)}) copy-start(bf16[512,4096]{1,0:T(8,128)(2,1)} %all-reduce.2.cloned.1.call-done) | copy-start | bytes 12582916
  230.8 146.4 %copy-start.4 = (f32[512]{0:T(512)}, f32[512]{0:T(512)S(1)}, u32[]{:S(2)}) copy-start(f32[512]{0:T(512)S(1)} %get-tuple-element.12) | copy-start | bytes 6148
  336.8 40.4 %copy-start.1 = (bf16[344,4096]{1,0:T(8,128)(2,1)S(1)}, bf16[344,4096]{1,0:T(8,128)(2,1)}, u32[]{:S(2)}) copy-start(bf16[344,4096]{1,0:T(8,128)(2,1)} %param.11) | copy-start | bytes 8454148
Sparse Core Ops, SparseCore 0:
  21.5 105.1 all-reduce.1
  232.2 104.5 all-gather.1
where the time goes:
time: 385 us; the launch traced here: 384 us
  waiting for transfers between devices  209 us (54%)
  blocking collectives  89.3 us (23%)
  local copies, waits for them, and re-layouts  41.9 us (11%)
  matrix products  21.7 us (6%)
  between operations  14.1 us (4%)
  other arithmetic  8.12 us (2%)
    psum x1, waiting for transfers between devices, device_step(): mlp_out = lax.psum(part_sum, 'tp')  105 us
    all_gather x1, waiting for transfers between devices, device_step(): log_probs = lax.all_gather(local_probs, 'tp', axis=1, tiled=True)  104 us
    pmax x1, blocking collectives, device_step(): row_max = lax.pmax(jnp.max(logits, axis=-1), 'tp')  45.7 us
    psum x1, blocking collectives, device_step(): row_stats = lax.psum(local_stats, 'tp')  43.6 us
    unnamed x17, local copies, waits for them, and re-layouts  41.9 us
    dot_general x1, matrix products, device_step(): jnp.dot(hidden_act, w_down, preferred_element_type=jnp.float32)  9.13 us
    dot_general x1, matrix products, device_step(): jnp.dot(normed, w_vocab, preferred_element_type=jnp.float32)  7.71 us
  transfers between devices with their start and end apart: 2, of which 2 were waited for; matrix products, arithmetic and copies ran while one was open for 0% of the time, Pallas kernels for 0%

commit v1 on v0

v1 whole, which is shorter than its diff:
```python
import functools
import math

import jax
import jax.numpy as jnp
from jax import lax
from jax.experimental import pallas as pl
from jax.experimental.pallas import tpu as pltpu
from jax.sharding import PartitionSpec as P

NORM_EPS = 1e-6
MESH = pl.DeviceIdType.MESH
NT = (((1,), (1,)), ((), ()))
PIECE = 1024
CHUNK = 256
SUB = 64


def place(side):
    me = lax.axis_index("tp")
    c = lax.rem(me, 2)
    chip = lax.div(me, 2)
    x, y = lax.rem(chip, side), lax.div(chip, side)
    i = x * (1 - c) + y * c
    j = y * (1 - c) + x * c
    s1 = 2 + (2 * side - 2) * c
    s2 = 2 * side - (2 * side - 2) * c

    def dev(a, b):
        return a * s1 + b * s2 + c

    nxt = lambda v: lax.rem(v + 1, side)
    prv = lambda v: lax.rem(v + side - 1, side)
    return me, c, i, j, dev(nxt(i), j), dev(prv(i), j), dev(i, nxt(j)), dev(i, prv(j)), me + 1 - 2 * c


def remote(src, dst, sems, k, to):
    return pltpu.make_async_remote_copy(
        src_ref=src, dst_ref=dst, send_sem=sems[0].at[k], recv_sem=sems[1].at[k],
        device_id={"tp": to}, device_id_type=MESH)


def sum_kernel(side, y_hbm, h_hbm, gain, x, Y, P0, T1a, T1b, T2a, T2b, H, lsem, ssem, rsem):
    me, c, i, j, R1, L1, R2, L2, PT = place(side)
    sems = (ssem, rsem)
    n1 = Y.shape[1] // 2
    n2 = n1 // side
    n3 = n2 // side
    pieces = Y.shape[0]
    half = pieces // 2

    base = pl.multiple_of(c * n1, n1)
    other = pl.multiple_of((1 - c) * n1, n1)
    row1 = lambda g: pl.multiple_of(c * n1 + g * n2, n2)
    row2 = lambda g: pl.multiple_of(c * n1 + i * n2 + g * n3, n3)
    mine = row2(j)

    loads = []
    for k, lo in enumerate((other, base)):
        for p in range(pieces):
            loads.append(pltpu.make_async_copy(
                y_hbm.at[pl.ds(lo, n1), pl.ds(p * PIECE, PIECE)], Y.at[p, pl.ds(lo, n1)], lsem.at[k * pieces + p]))
    for p in range(pieces):
        loads.append(pltpu.make_async_copy(
            h_hbm.at[pl.ds(mine, n3), pl.ds(p * PIECE, PIECE)], H.at[p], lsem.at[2 * pieces + p]))
    for cp in loads:
        cp.start()

    barrier = pltpu.get_barrier_semaphore()
    for to in (R1, L1, R2, L2, PT):
        pl.semaphore_signal(barrier, inc=1, device_id={"tp": to}, device_id_type=MESH)
    pl.semaphore_wait(barrier, 5)

    sent = []

    def start(cp):
        cp.start()
        sent.append(cp)
        return cp

    swaps = []
    for p in range(pieces):
        loads[p].wait()
        swaps.append(start(remote(Y.at[p, pl.ds(other, n1)], P0.at[p], sems, p, PT)))
    for cp in loads[pieces:]:
        cp.wait()

    f32 = lambda v: v.astype(jnp.float32)
    for p in range(pieces):
        swaps[p].wait_recv()
    nxt = lambda v: lax.rem(v + 1, side)
    prv = lambda v: lax.rem(v + side - 1, side)
    opp = lambda v: lax.rem(v + 2, side)

    def add_partner(g):
        def body(p, _):
            at = pl.ds(row1(g), n2)
            Y[p, at] = (f32(Y[p, at]) + f32(P0[p, pl.ds(pl.multiple_of(g * n2, n2), n2)])).astype(jnp.bfloat16)
            return 0
        lax.fori_loop(0, pieces, body, 0)

    def ring_sum(pos, row, n, R, L, Ta, Tb, k, prepare):
        prepare(opp(pos))
        lo, hi = pl.ds(0, half), pl.ds(half, half)
        far = pl.ds(row(opp(pos)), n)
        m0 = start(remote(Y.at[lo, far], Ta.at[0], sems, k, R))
        m1 = start(remote(Y.at[hi, far], Ta.at[1], sems, k + 1, L))
        prepare(nxt(pos))
        prepare(prv(pos))
        right, left = pl.ds(row(nxt(pos)), n), pl.ds(row(prv(pos)), n)
        m0.wait_recv()
        for p in range(half):
            Y[p, right] = (f32(Y[p, right]) + f32(Ta[0, p])).astype(jnp.bfloat16)
        m2 = start(remote(Y.at[:, right], Tb.at[0], sems, k + 2, R))
        m1.wait_recv()
        for p in range(half):
            Y[half + p, left] = (f32(Y[half + p, left]) + f32(Ta[1, p])).astype(jnp.bfloat16)
        m3 = start(remote(Y.at[:, left], Tb.at[1], sems, k + 3, L))
        prepare(pos)
        m2.wait_recv()
        m3.wait_recv()

    ring_sum(i, row1, n2, R1, L1, T1a, T1b, 4, add_partner)
    own = pl.ds(row1(i), n2)
    for p in range(pieces):
        Y[p, own] = (f32(Y[p, own]) + f32(T1b[0, p]) + f32(T1b[1, p])).astype(jnp.bfloat16)
    ring_sum(j, row2, n3, R2, L2, T2a, T2b, 8, lambda g: None)

    at = pl.ds(mine, n3)
    total = jnp.zeros((n3, 1), jnp.float32)
    rs = []
    for p in range(pieces):
        r = f32(H[p]) + (f32(Y[p, at]) + f32(T2b[0, p]) + f32(T2b[1, p]))
        rs.append(r)
        total += jnp.sum(r * r, axis=-1, keepdims=True)
    inv = lax.rsqrt(total / (pieces * PIECE) + NORM_EPS)
    for p in range(pieces):
        x[p, at] = (gain[0:1, p * PIECE:(p + 1) * PIECE] * rs[p] * inv).astype(jnp.bfloat16)

    def ring_gather(pos, row, n, R, L, k):
        lo, hi = pl.ds(0, half), pl.ds(half, half)
        own = x.at[:, pl.ds(row(pos), n)]
        left, right, far = row(prv(pos)), row(nxt(pos)), row(opp(pos))
        at = lambda r, ps=slice(None): x.at[ps, pl.ds(r, n)]
        start(remote(own, own, sems, k, R))
        start(remote(own, own, sems, k + 1, L))
        remote(at(left), at(left), sems, k, R).wait_recv()
        start(remote(at(left, lo), at(left, lo), sems, k + 2, R))
        remote(at(right), at(right), sems, k + 1, L).wait_recv()
        start(remote(at(right, hi), at(right, hi), sems, k + 3, L))
        yield left
        yield right
        remote(at(far, lo), at(far, lo), sems, k + 2, R).wait_recv()
        remote(at(far, hi), at(far, hi), sems, k + 3, L).wait_recv()
        yield far

    for _ in ring_gather(j, row2, n3, R2, L2, 12):
        pass
    k = 20
    line = x.at[:, pl.ds(row1(i), n2)]
    start(remote(line, line, sems, k, PT))
    for r in ring_gather(i, row1, n2, R1, L1, 16):
        k += 1
        line = x.at[:, pl.ds(r, n2)]
        start(remote(line, line, sems, k, PT))
    ip = j
    rowp = lambda g: pl.multiple_of((1 - c) * n1 + g * n2, n2)
    for k, g in enumerate((ip, prv(ip), nxt(ip), opp(ip))):
        line = x.at[:, pl.ds(rowp(g), n2)]
        remote(line, line, sems, 20 + k, PT).wait_recv()
    for cp in sent:
        cp.wait_send()


def head_kernel(side, n_dev, v_loc, x, wv_hbm, temp, target, G, out, WV, LT, LP, ST, wsem, ssem, rsem, stsem, strsem):
    me, c, i, j, R1, L1, R2, L2, PT = place(side)
    rows = x.shape[1]
    pieces = x.shape[0]
    vpad = WV.shape[1]
    chunks = rows // CHUNK
    subs = rows // SUB
    nxt = lambda v: lax.rem(v + 1, side)
    prv = lambda v: lax.rem(v + side - 1, side)
    opp = lambda v: lax.rem(v + 2, side)

    wloads = [pltpu.make_async_copy(
        wv_hbm.at[:, pl.ds(p * PIECE, PIECE)], WV.at[p, pl.ds(0, v_loc)], wsem.at[p]) for p in range(pieces)]
    for cp in wloads:
        cp.start()
    barrier = pltpu.get_barrier_semaphore()

    def greet(t, _):
        to = lax.rem(me + 1 + t, n_dev)
        pl.semaphore_signal(barrier, inc=1, device_id={"tp": to}, device_id_type=MESH)
        return 0
    lax.fori_loop(0, n_dev - 1, greet, 0)
    for p in range(pieces):
        WV[p, v_loc:] = jnp.zeros((vpad - v_loc, PIECE), WV.dtype)
    for cp in wloads:
        cp.wait()

    vid = lax.broadcasted_iota(jnp.int32, (vpad, CHUNK), 0)
    for k in range(chunks):
        at = pl.ds(k * CHUNK, CHUNK)
        acc = lax.dot_general(WV[0], x[0, at], NT, preferred_element_type=jnp.float32)
        for p in range(1, pieces):
            acc += lax.dot_general(WV[p], x[p, at], NT, preferred_element_type=jnp.float32)
        l = acc / temp[0:1, k * CHUNK:(k + 1) * CHUNK]
        LT[k] = l
        real = vid < v_loc
        m = jnp.max(jnp.where(real, l, -jnp.inf), axis=0, keepdims=True)
        e = jnp.where(real, jnp.exp(l - m), 0.0)
        s = jnp.sum(e, axis=0, keepdims=True)
        w = jnp.sum(e * l, axis=0, keepdims=True)
        ids = target[0:1, k * CHUNK:(k + 1) * CHUNK] - me * v_loc
        t = jnp.sum(jnp.where((vid == ids) & real, l, 0.0), axis=0, keepdims=True)
        both = [v[:, h * 128:(h + 1) * 128] for h in range(CHUNK // 128) for v in (m, s, w, t)]
        ST[k, me] = jnp.concatenate(both, axis=0)
        if k == 0:
            pl.semaphore_wait(barrier, n_dev - 1)

        def tell(t, _, k=k):
            to = lax.rem(me + 1 + t, n_dev)
            pltpu.make_async_remote_copy(
                src_ref=ST.at[k, me], dst_ref=ST.at[k, me], send_sem=stsem.at[k, t], recv_sem=strsem.at[k, t],
                device_id={"tp": to}, device_id_type=MESH).start()
            return 0
        lax.fori_loop(0, n_dev - 1, tell, 0)

    def heard(k, wait):
        def body(t, _):
            frm = lax.rem(me + n_dev - 1 - t, n_dev)
            cp = pltpu.make_async_remote_copy(
                src_ref=ST.at[k, me], dst_ref=ST.at[k, frm], send_sem=stsem.at[k, t], recv_sem=strsem.at[k, t],
                device_id={"tp": frm}, device_id_type=MESH)
            wait(cp)
            return 0
        lax.fori_loop(0, n_dev - 1, body, 0)

    sems = (ssem, rsem)
    sent = []

    def start(cp):
        cp.start()
        sent.append(cp)

    lo, hi = pl.ds(0, SUB // 2), pl.ds(SUB // 2, SUB // 2)

    def own(k):
        b = G.at[c, i, j, pl.ds(k * SUB, SUB)]
        start(remote(b, b, sems, 12 * k, R1))
        start(remote(b, b, sems, 12 * k + 1, L1))

    def blk(a, b, k, part=None):
        if part is None:
            return G.at[c, a, b, pl.ds(k * SUB, SUB)]
        return G.at[c, a, b, pl.ds(k * SUB + part * (SUB // 2), SUB // 2)]

    def first(k):
        left, right = prv(i), nxt(i)
        remote(blk(left, j, k), blk(left, j, k), sems, 12 * k, R1).wait_recv()
        b = blk(left, j, k, 0)
        start(remote(b, b, sems, 12 * k + 2, R1))
        remote(blk(right, j, k), blk(right, j, k), sems, 12 * k + 1, L1).wait_recv()
        b = blk(right, j, k, 1)
        start(remote(b, b, sems, 12 * k + 3, L1))

    def line(b, k, a0=0, na=side):
        return G.at[c, pl.ds(a0, na), b, pl.ds(k * SUB, SUB)]

    def second(k):
        far = opp(i)
        for part in range(2):
            b = blk(far, j, k, part)
            remote(b, b, sems, 12 * k + 2 + part, R1).wait_recv()
        b = line(j, k)
        start(remote(b, b, sems, 12 * k + 4, R2))
        start(remote(b, b, sems, 12 * k + 5, L2))
        start(remote(b, b, sems, 12 * k + 8, PT))

    def third(k):
        b = line(prv(j), k)
        remote(b, b, sems, 12 * k + 4, R2).wait_recv()
        b2 = line(prv(j), k, 0, side // 2)
        start(remote(b2, b2, sems, 12 * k + 6, R2))
        start(remote(b, b, sems, 12 * k + 9, PT))
        b = line(nxt(j), k)
        remote(b, b, sems, 12 * k + 5, L2).wait_recv()
        b2 = line(nxt(j), k, side // 2, side // 2)
        start(remote(b2, b2, sems, 12 * k + 7, L2))
        start(remote(b, b, sems, 12 * k + 10, PT))

    def fourth(k):
        for part in range(2):
            b = line(opp(j), k, part * (side // 2), side // 2)
            remote(b, b, sems, 12 * k + 6 + part, R2).wait_recv()
        b = line(opp(j), k)
        start(remote(b, b, sems, 12 * k + 11, PT))

    def last(k):
        jp = i
        for q, g in enumerate((jp, prv(jp), nxt(jp), opp(jp))):
            b = G.at[1 - c, :, g, pl.ds(k * SUB, SUB)]
            remote(b, b, sems, 12 * k + 8 + q, PT).wait_recv()

    per = CHUNK // SUB
    step = 0

    def advance(limit):
        nonlocal step
        while step < limit:
            own(step)
            for lag, act in ((1, first), (2, second), (3, third), (4, fourth), (5, last)):
                if step >= lag:
                    act(step - lag)
            step += 1

    for k in range(chunks):
        heard(k, lambda cp: cp.wait_recv())
        st = ST[k]
        for h in range(CHUNK // 128):
            b = 4 * h
            ms, ss, ws, ts = (st[:, b + q:b + q + 1, :] for q in range(4))
            m = jnp.max(ms, axis=0)
            f = jnp.exp(ms - m[None])
            s = jnp.sum(ss * f, axis=0)
            w = jnp.sum(ws * f, axis=0)
            t = jnp.sum(ts, axis=0)
            ln = m + jnp.log(s)
            cols = pl.ds(k * CHUNK + h * 128, 128)
            out[0:1, cols] = ln
            out[1:2, cols] = ln - w / s
            out[2:3, cols] = t - ln
            LP[...] = LT[k, :, h * 128:(h + 1) * 128] - ln

            def turn(q, _, k=k, h=h):
                v = pl.ds(pl.multiple_of(q * 128, 128), 128)
                G[c, i, j, pl.ds(k * CHUNK + h * 128, 128), v] = LP[v].T.astype(jnp.bfloat16)
                return 0
            lax.fori_loop(0, vpad // 128, turn, 0)
            advance(k * per + (h + 1) * 128 // SUB)
    for k in range(subs, subs + 5):
        for lag, act in ((1, first), (2, second), (3, third), (4, fourth), (5, last)):
            if lag <= k and k - lag < subs:
                act(k - lag)
    for k in range(chunks):
        heard(k, lambda cp: cp.wait_send())
    for cp in sent:
        cp.wait_send()


def layout_kernel(side, v_loc, g, o):
    r = pl.ds(pl.multiple_of(pl.program_id(0) * o.shape[0], o.shape[0]), o.shape[0])
    for fam in range(2):
        for a in range(side):
            for b in range(side):
                d = ((b * side + a) * 2) if fam == 0 else ((a * side + b) * 2 + 1)
                o[:, d * v_loc:(d + 1) * v_loc] = g[fam, a, b, r, 0:v_loc]


def solution(mesh):
    n_dev = mesh.shape["tp"]
    side = math.isqrt(n_dev // 2)

    def device_step(hidden, w_gate, w_up, w_down, norm_gain, w_vocab, temperature, target):
        rows, d = hidden.shape
        v_loc = w_vocab.shape[1]
        pieces = d // PIECE
        vpad = -(-v_loc // 128) * 128
        gate_pre = jnp.dot(hidden, w_gate, preferred_element_type=jnp.float32)
        up_pre = jnp.dot(hidden, w_up, preferred_element_type=jnp.float32)
        hidden_act = (jax.nn.silu(gate_pre) * up_pre).astype(jnp.bfloat16)
        part_sum = jnp.dot(hidden_act, w_down, preferred_element_type=jnp.float32).astype(jnp.bfloat16)

        n1 = rows // 2
        n2, n3 = n1 // side, n1 // side // side
        vm = pl.BlockSpec(memory_space=pltpu.VMEM)
        hbm = pl.BlockSpec(memory_space=pl.ANY)
        bf = jnp.bfloat16
        x = pl.pallas_call(
            functools.partial(sum_kernel, side),
            out_shape=pltpu.VMEM((pieces, rows, PIECE), bf),
            in_specs=[hbm, hbm, vm],
            out_specs=vm,
            scratch_shapes=[
                pltpu.VMEM((pieces, rows, PIECE), bf),
                pltpu.VMEM((pieces, n1, PIECE), bf),
                pltpu.VMEM((2, pieces // 2, n2, PIECE), bf),
                pltpu.VMEM((2, pieces, n2, PIECE), bf),
                pltpu.VMEM((2, pieces // 2, n3, PIECE), bf),
                pltpu.VMEM((2, pieces, n3, PIECE), bf),
                pltpu.VMEM((pieces, n3, PIECE), bf),
                pltpu.SemaphoreType.DMA((3 * pieces,)),
                pltpu.SemaphoreType.DMA((24,)),
                pltpu.SemaphoreType.DMA((24,)),
            ],
            compiler_params=pltpu.CompilerParams(
                collective_id=0, has_side_effects=True, vmem_limit_bytes=20 << 20),
            name="sum_norm",
        )(part_sum, hidden, norm_gain.reshape(1, d))

        chunks, subs = rows // CHUNK, rows // SUB
        g, stats = pl.pallas_call(
            functools.partial(head_kernel, side, n_dev, v_loc),
            out_shape=(pltpu.VMEM((2, side, side, rows, vpad), bf), pltpu.VMEM((8, rows), jnp.float32)),
            in_specs=[vm, hbm, vm, vm],
            out_specs=(vm, vm),
            scratch_shapes=[
                pltpu.VMEM((pieces, vpad, PIECE), bf),
                pltpu.VMEM((chunks, vpad, CHUNK), jnp.float32),
                pltpu.VMEM((vpad, 128), jnp.float32),
                pltpu.VMEM((chunks, n_dev, 8, 128), jnp.float32),
                pltpu.SemaphoreType.DMA((pieces,)),
                pltpu.SemaphoreType.DMA((12 * subs,)),
                pltpu.SemaphoreType.DMA((12 * subs,)),
                pltpu.SemaphoreType.DMA((chunks, n_dev - 1)),
                pltpu.SemaphoreType.DMA((chunks, n_dev - 1)),
            ],
            compiler_params=pltpu.CompilerParams(
                collective_id=1, has_side_effects=True, vmem_limit_bytes=24 << 20),
            name="head",
        )(x, w_vocab.T, temperature.reshape(1, rows), target.reshape(1, rows))

        step = 32
        log_probs = pl.pallas_call(
            functools.partial(layout_kernel, side, v_loc),
            out_shape=jax.ShapeDtypeStruct((rows, n_dev * v_loc), bf),
            grid=(rows // step,),
            in_specs=[vm],
            out_specs=pl.BlockSpec((step, n_dev * v_loc), lambda s: (s, 0)),
            compiler_params=pltpu.CompilerParams(vmem_limit_bytes=16 << 20),
            name="layout",
        )(g)
        return stats[0], stats[1], stats[2], log_probs

    return jax.shard_map(
        device_step,
        mesh=mesh,
        in_specs=(P("dp", None), P(None, "tp"), P(None, "tp"), P("tp", None), P(None),
                  P(None, "tp"), P("dp"), P("dp")),
        out_specs=(P("dp"), P("dp"), P("dp"), P("dp", None)),
        check_vma=False,
    )
```

time: 385 us -> 209 us (0.54)
  waiting for transfers between devices: 209 us -> 0 us
  Pallas kernels: 0 us -> 187 us
  blocking collectives: 89.3 us -> 0 us
  local copies, waits for them, and re-layouts: 41.9 us -> 7 us
  between operations: 14.1 us -> 0.69 us
  other arithmetic: 8.12 us -> 0 us
  matrix products: 21.7 us -> 14 us
    pallas_call x0 -> x3, Pallas kernels: none -> 187 us  [the longest x1 113 us: device_step(): pl.pallas_call(functools.partial(head_kernel, side, n_dev, v_loc), out_sh...]
    psum x1 -> x0, waiting for transfers between devices: 105 us -> none  [device_step(): mlp_out = lax.psum(part_sum, 'tp')]
    all_gather x1 -> x0, waiting for transfers between devices: 104 us -> none  [device_step(): log_probs = lax.all_gather(local_probs, 'tp', axis=1, tiled=True)]
    pmax x1 -> x0, blocking collectives: 45.7 us -> none  [device_step(): row_max = lax.pmax(jnp.max(logits, axis=-1), 'tp')]
    psum x1 -> x0, blocking collectives: 43.6 us -> none  [device_step(): row_stats = lax.psum(local_stats, 'tp')]
    unnamed x17 -> x12, local copies, waits for them, and re-layouts: 41.9 us -> 6.4 us
    dot_general x1 -> x0, matrix products: 7.71 us -> none  [device_step(): jnp.dot(normed, w_vocab, preferred_element_type=jnp.float32)]
    reduce_sum x2 -> x0, other arithmetic: 5.7 us -> none  [the longest x1 5.03 us: device_step(): jnp.mean(residual * residual, axis=-1, keepdims=True) + NORM_EPS]
  transfers between devices with their start and end apart: 2 -> 0, of which waited for: 2 -> 0; matrix products, arithmetic and copies ran while one was open for 0% -> 0% of each run, Pallas kernels for 0% -> 0%
where the time goes in v1:
time: 209 us; the launch traced here: 208 us
  Pallas kernels  187 us (89%)
  matrix products  14 us (7%)
  local copies, waits for them, and re-layouts  7 us (3%)
    pallas_call x1, Pallas kernels, device_step(): pl.pallas_call(functools.partial(head_kernel, side, n_dev, v_loc), out_sh...  113 us
    pallas_call x1, Pallas kernels, device_step(): pl.pallas_call(functools.partial(sum_kernel, side), out_shape=pltpu.VMEM(...  57.7 us
    pallas_call x1, Pallas kernels, device_step(): pl.pallas_call(functools.partial(layout_kernel, side, v_loc), out_shape=j...  15.7 us
    dot_general x1, matrix products, device_step(): jnp.dot(hidden_act, w_down, preferred_element_type=jnp.float32)  9.13 us
    unnamed x12, local copies, waits for them, and re-layouts  6.4 us
    dot_general x1, matrix products, device_step(): gate_pre = jnp.dot(hidden, w_gate, preferred_element_type=jnp.float32)  4.86 us

profile of v1, /device:TPU:97, one launch (start us, length us, event | category | flops | bytes accessed | tf_op | source)
XLA Modules:
  0.0 208.5 jit_solution(1123984456486079639)
XLA Ops:
  0.6 0.0 copy-start
  0.6 4.9 %fusion.4 = f32[512,344]{0,1:T(8,128)S(1)} fusion(bf16[512,4096]{1,0:T(8,128)(2,1)} %h_hbm.1, bf16[4096,344]{0,1:T(8,128)(2,1)} %param.9), kind=kOutput, calls=%fused_computation.6 | convolution fusion | flops 1442840576 | bytes 7716864 | tf_op jit(solution)/shard_map/dot_general | solution.py:370
  5.5 0.0 copy-done
  5.5 0.0 copy-start.5
  5.5 9.1 %convolution_convert_fusion.y_hbm = bf16[512,4096]{1,0:T(8,128)(2,1)} fusion(bf16[344,4096]{1,0:T(8,128)(2,1)S(1)} %copy-done, bf16[512,4096]{1,0:T(8,128)(2,1)} %h_hbm.1, bf16[4096,344]{0,1:T(8,128)(2,1)} %param.10, f32[512,344]{0,1:T(8,128)S(1)} %fusion.4), kind=kOutput, calls=%fused_computation | convolution fusion | flops 2888835072 | bytes 14729216 | tf_op jit(solution)/shard_map/dot_general | solution.py:373
  14.7 0.0 copy-done.5
  14.7 0.0 copy-start.3
  14.7 2.2 %copy-done.3 = bf16[512,4096]{1,0:T(8,128)(2,1)S(1)} copy-done((bf16[512,4096]{1,0:T(8,128)(2,1)S(1)}, bf16[512,4096]{1,0:T(8,128)(2,1)}, u32[]{:S(2)}) %copy-start.3) | copy-done | bytes 4194328
  16.9 0.0 copy-start.4
  16.9 2.2 %copy-done.4 = bf16[512,4096]{1,0:T(8,128)(2,1)S(1)} copy-done((bf16[512,4096]{1,0:T(8,128)(2,1)S(1)}, bf16[512,4096]{1,0:T(8,128)(2,1)}, u32[]{:S(2)}) %copy-start.4) | copy-done | bytes 4194328
  19.0 57.7 %sum_norm.1.x = bf16[4,512,1024]{2,1,0:T(8,128)(2,1)S(1)} custom-call(bf16[512,4096]{1,0:T(8,128)(2,1)S(1)} %copy-done.4, bf16[512,4096]{1,0:T(8,128)(2,1)S(1)} %copy-done.3, f32[1,4096]{1,0:T(1,128)S(1)} %bitcast.12), custom_call_target="tpu_custom_call" | custom-call | tf_op jit(solution)/shard_map/sum_norm/pallas_call | solution.py:380
  76.7 0.0 copy-start.2
  76.7 2.0 copy-done.2
  78.7 113.5 %head.1 = (bf16[2,4,4,512,1024]{4,3,2,1,0:T(8,128)(2,1)S(1)}, f32[8,512]{1,0:T(8,128)S(1)}) custom-call(bf16[4,512,1024]{2,1,0:T(8,128)(2,1)} %copy-done.2, bf16[1000,4096]{1,0:T(8,128)(2,1)} %bitcast.13, f32[1,512]{1,0:T(1,128)} %bitcast.17, s32[1,512]{1,0:T(1,128)} %bitcast.18), custom_call_target="tpu_custom_call" | custom-call | tf_op jit(solution)/shard_map/head/pallas_call | solution.py:403
  192.2 0.6 fusion.3
  192.8 0.0 copy-start.1
  192.8 15.7 %layout.1 = bf16[512,32000]{1,0:T(8,128)(2,1)} custom-call(bf16[2,4,4,512,1024]{4,3,2,1,0:T(8,128)(2,1)S(1)} %get-tuple-element.7.g), custom_call_target="tpu_custom_call" | custom-call | tf_op jit(solution)/shard_map/layout/pallas_call | solution.py:425
  208.4 0.0 copy-done.1
Async XLA Ops:
  0.6 4.9 %copy-start = (bf16[344,4096]{1,0:T(8,128)(2,1)S(1)}, bf16[344,4096]{1,0:T(8,128)(2,1)}, u32[]{:S(2)}) copy-start(bf16[344,4096]{1,0:T(8,128)(2,1)} %param.11) | copy-start | bytes 8454148
  5.5 9.1 %copy-start.5 = (f32[4096]{0:T(1024)S(1)}, f32[4096]{0:T(1024)}, u32[]{:S(2)}) copy-start(f32[4096]{0:T(1024)} %param.12) | copy-start | bytes 49156
  14.7 2.2 %copy-start.3 = (bf16[512,4096]{1,0:T(8,128)(2,1)S(1)}, bf16[512,4096]{1,0:T(8,128)(2,1)}, u32[]{:S(2)}) copy-start(bf16[512,4096]{1,0:T(8,128)(2,1)} %h_hbm.1) | copy-start | bytes 12582916
  16.9 2.2 %copy-start.4 = (bf16[512,4096]{1,0:T(8,128)(2,1)S(1)}, bf16[512,4096]{1,0:T(8,128)(2,1)}, u32[]{:S(2)}) copy-start(bf16[512,4096]{1,0:T(8,128)(2,1)} %convolution_convert_fusion.y_hbm) | copy-start | bytes 12582916
  76.7 2.0 copy-start.2
  192.8 15.7 %copy-start.1 = (bf16[344,4096]{1,0:T(8,128)(2,1)S(1)}, bf16[344,4096]{1,0:T(8,128)(2,1)}, u32[]{:S(2)}) copy-start(bf16[344,4096]{1,0:T(8,128)(2,1)} %param.11) | copy-start | bytes 8454148

commit v2 on v0

v2 whole, which is shorter than its diff:
```python
import functools
import math

import jax
import jax.numpy as jnp
from jax import lax
from jax.experimental import pallas as pl
from jax.experimental.pallas import tpu as pltpu
from jax.sharding import PartitionSpec as P

NORM_EPS = 1e-6
MESH = pl.DeviceIdType.MESH
NT = (((1,), (1,)), ((), ()))
PIECE = 1024
CHUNK = 256
SUB = 128


def place(side):
    me = lax.axis_index("tp")
    c = lax.rem(me, 2)
    chip = lax.div(me, 2)
    x, y = lax.rem(chip, side), lax.div(chip, side)
    i = x * (1 - c) + y * c
    j = y * (1 - c) + x * c
    s1 = 2 + (2 * side - 2) * c
    s2 = 2 * side - (2 * side - 2) * c

    def dev(a, b):
        return a * s1 + b * s2 + c

    nxt = lambda v: lax.rem(v + 1, side)
    prv = lambda v: lax.rem(v + side - 1, side)
    return me, c, i, j, dev(nxt(i), j), dev(prv(i), j), dev(i, nxt(j)), dev(i, prv(j)), me + 1 - 2 * c


def remote(src, dst, sems, k, to):
    return pltpu.make_async_remote_copy(
        src_ref=src, dst_ref=dst, send_sem=sems[0].at[k], recv_sem=sems[1].at[k],
        device_id={"tp": to}, device_id_type=MESH)


def tail_kernel(side, n_dev, f_loc, v_loc, h_hbm, wg_hbm, wu_hbm, wd_hbm, gain, wv_hbm, temp, target, G, out,
                H, W, WD, X, WV, LT, LP, ST, lsem, ssem, rsem, gssem, grsem, stsem, strsem):
    me, c, i, j, R1, L1, R2, L2, PT = place(side)
    rows, d = H.shape
    vpad = WV.shape[0]
    fpad = WD.shape[0]
    pieces = d // PIECE
    half = pieces // 2
    chunks = rows // CHUNK
    subs = rows // SUB
    n1 = CHUNK // 2
    n2 = n1 // side
    n3 = n2 // side
    f32 = lambda v: v.astype(jnp.float32)
    bf16 = lambda v: v.astype(jnp.bfloat16)
    nxt = lambda v: lax.rem(v + 1, side)
    prv = lambda v: lax.rem(v + side - 1, side)
    opp = lambda v: lax.rem(v + 2, side)

    loads = {}

    def load(name, src, dst):
        cp = pltpu.make_async_copy(src, dst, lsem.at[len(loads)])
        cp.start()
        loads[name] = cp

    load("h0", h_hbm.at[pl.ds(0, CHUNK)], H.at[pl.ds(0, CHUNK)])
    load("wg", wg_hbm, W.at[pl.ds(0, f_loc)])
    load("wu", wu_hbm, W.at[pl.ds(fpad, f_loc)])
    load("wd", wd_hbm, WD.at[pl.ds(0, f_loc)])
    for b in range(1, chunks):
        load("h%d" % b, h_hbm.at[pl.ds(b * CHUNK, CHUNK)], H.at[pl.ds(b * CHUNK, CHUNK)])
    load("wv", wv_hbm, WV.at[pl.ds(0, v_loc)])

    barrier = pltpu.get_barrier_semaphore()

    def greet(t, _):
        to = lax.rem(me + 1 + t, n_dev)
        pl.semaphore_signal(barrier, inc=1, device_id={"tp": to}, device_id_type=MESH)
        return 0
    lax.fori_loop(0, n_dev - 1, greet, 0)
    W[f_loc:fpad] = jnp.zeros((fpad - f_loc, d), W.dtype)
    W[fpad + f_loc:] = jnp.zeros((fpad - f_loc, d), W.dtype)
    WD[f_loc:] = jnp.zeros((fpad - f_loc, d), WD.dtype)
    WV[v_loc:] = jnp.zeros((vpad - v_loc, d), WV.dtype)

    sent = []

    def start(cp):
        cp.start()
        sent.append(cp)
        return cp

    Y = G.at[0, 0]

    def mlp(b):
        gu = lax.dot_general(W[...], H[b * CHUNK:(b + 1) * CHUNK], NT, preferred_element_type=jnp.float32)
        g, u = gu[:fpad], gu[fpad:]
        a = bf16((g * lax.logistic(g) * u).T)
        if b == 0:
            loads["wd"].wait()
            pl.semaphore_wait(barrier, n_dev - 1)
        for p in range(pieces):
            Y[p, b * CHUNK:(b + 1) * CHUNK] = bf16(
                jnp.dot(a, WD[:, p * PIECE:(p + 1) * PIECE], preferred_element_type=jnp.float32))
            theirs = Y.at[p, pl.ds(pl.multiple_of(b * CHUNK + (1 - c) * n1, n1), n1)]
            start(remote(theirs, G.at[0, 1, p, pl.ds(b * n1, n1)], (ssem, rsem), 24 * b + p, PT))

    def chain(b):
        sems = (ssem, rsem)
        k0 = 24 * b
        P0 = G.at[0, 1]
        T = G.at[1, b]
        lo, hi, every = pl.ds(0, half), pl.ds(half, half), pl.ds(0, pieces)
        row1 = lambda g: pl.multiple_of(b * CHUNK + c * n1 + g * n2, n2)
        row2 = lambda g: pl.multiple_of(b * CHUNK + c * n1 + i * n2 + g * n3, n3)

        def add_partner(g):
            at = pl.ds(row1(g), n2)
            frm = pl.ds(pl.multiple_of(b * n1 + g * n2, n2), n2)
            for p in range(pieces):
                Y[p, at] = bf16(f32(Y[p, at]) + f32(P0[p, frm]))

        def ring_sum(pos, row, n, R, L, t0, k, prepare):
            ta, tl, tr = pl.ds(t0, n), pl.ds(t0 + n, n), pl.ds(t0 + 2 * n, n)
            prepare(opp(pos))
            far = pl.ds(row(opp(pos)), n)
            m0 = start(remote(Y.at[lo, far], T.at[lo, ta], sems, k, R))
            m1 = start(remote(Y.at[hi, far], T.at[hi, ta], sems, k + 1, L))
            prepare(nxt(pos))
            prepare(prv(pos))
            right, left = pl.ds(row(nxt(pos)), n), pl.ds(row(prv(pos)), n)
            yield
            m0.wait_recv()
            for p in range(half):
                Y[p, right] = bf16(f32(Y[p, right]) + f32(T[p, ta]))
            m2 = start(remote(Y.at[every, right], T.at[every, tl], sems, k + 2, R))
            m1.wait_recv()
            for p in range(half, pieces):
                Y[p, left] = bf16(f32(Y[p, left]) + f32(T[p, ta]))
            m3 = start(remote(Y.at[every, left], T.at[every, tr], sems, k + 3, L))
            prepare(pos)
            yield
            m2.wait_recv()
            m3.wait_recv()
            own = pl.ds(row(pos), n)
            for p in range(pieces):
                total = f32(Y[p, own]) + f32(T[p, tl]) + f32(T[p, tr])
                yield p, total

        def drive(steps, keep):
            for got in steps:
                if got is None:
                    yield
                else:
                    keep(*got)

        yield
        for p in range(pieces):
            box = G.at[0, 1, p, pl.ds(b * n1, n1)]
            remote(box, box, sems, k0 + p, PT).wait_recv()
        own1 = pl.ds(row1(i), n2)

        def keep1(p, total):
            Y[p, own1] = bf16(total)
        yield from drive(ring_sum(i, row1, n2, R1, L1, 0, k0 + 4, add_partner), keep1)
        sums = []
        yield from drive(ring_sum(j, row2, n3, R2, L2, 3 * n2, k0 + 8, lambda g: None), lambda p, t: sums.append(t))

        mine = pl.ds(row2(j), n3)
        square = jnp.zeros((n3, 1), jnp.float32)
        for p in range(pieces):
            sums[p] = f32(H[mine, p * PIECE:(p + 1) * PIECE]) + sums[p]
            square += jnp.sum(sums[p] * sums[p], axis=-1, keepdims=True)
        inv = lax.rsqrt(square / d + NORM_EPS)
        for p in range(pieces):
            cols = slice(p * PIECE, (p + 1) * PIECE)
            X[mine, cols] = bf16(gain[0:1, cols] * sums[p] * inv)

        left_half, right_half = pl.ds(0, d // 2), pl.ds(d // 2, d // 2)

        def ring_gather(pos, row, n, R, L, k):
            at = lambda r, cols=pl.ds(0, d): X.at[pl.ds(r, n), cols]
            own, left, right, far = row(pos), row(prv(pos)), row(nxt(pos)), row(opp(pos))
            start(remote(at(own), at(own), sems, k, R))
            start(remote(at(own), at(own), sems, k + 1, L))
            yield own
            yield
            remote(at(left), at(left), sems, k, R).wait_recv()
            start(remote(at(left, left_half), at(left, left_half), sems, k + 2, R))
            remote(at(right), at(right), sems, k + 1, L).wait_recv()
            start(remote(at(right, right_half), at(right, right_half), sems, k + 3, L))
            yield left
            yield right
            yield
            remote(at(far, left_half), at(far, left_half), sems, k + 2, R).wait_recv()
            remote(at(far, right_half), at(far, right_half), sems, k + 3, L).wait_recv()
            yield far

        for got in ring_gather(j, row2, n3, R2, L2, k0 + 12):
            if got is None:
                yield
        k = k0 + 20
        for got in ring_gather(i, row1, n2, R1, L1, k0 + 16):
            if got is None:
                yield
            else:
                line = X.at[pl.ds(got, n2)]
                start(remote(line, line, sems, k, PT))
                k += 1
        yield
        for q, g in enumerate((j, prv(j), nxt(j), opp(j))):
            line = X.at[pl.ds(pl.multiple_of(b * CHUNK + (1 - c) * n1 + g * n2, n2), n2)]
            remote(line, line, sems, k0 + 20 + q, PT).wait_recv()

    vid = lax.broadcasted_iota(jnp.int32, (vpad, CHUNK), 0)

    def logits(b):
        cols = slice(b * CHUNK, (b + 1) * CHUNK)
        l = lax.dot_general(WV[...], X[cols], NT, preferred_element_type=jnp.float32) / temp[0:1, cols]
        LT[b] = l
        real = vid < v_loc
        m = jnp.max(jnp.where(real, l, -jnp.inf), axis=0, keepdims=True)
        e = jnp.where(real, jnp.exp(l - m), 0.0)
        s = jnp.sum(e, axis=0, keepdims=True)
        w = jnp.sum(e * l, axis=0, keepdims=True)
        ids = target[0:1, cols] - me * v_loc
        t = jnp.sum(jnp.where((vid == ids) & real, l, 0.0), axis=0, keepdims=True)
        both = [v[:, h * 128:(h + 1) * 128] for h in range(CHUNK // 128) for v in (m, s, w, t)]
        ST[b, me] = jnp.concatenate(both, axis=0)

    def tell(b):
        def body(t, _):
            to = lax.rem(me + 1 + t, n_dev)
            pltpu.make_async_remote_copy(
                src_ref=ST.at[b, me], dst_ref=ST.at[b, me], send_sem=stsem.at[b, t], recv_sem=strsem.at[b, t],
                device_id={"tp": to}, device_id_type=MESH).start()
            return 0
        lax.fori_loop(0, n_dev - 1, body, 0)

    def heard(b, wait):
        def body(t, _):
            frm = lax.rem(me + n_dev - 1 - t, n_dev)
            cp = pltpu.make_async_remote_copy(
                src_ref=ST.at[b, me], dst_ref=ST.at[b, frm], send_sem=stsem.at[b, t], recv_sem=strsem.at[b, t],
                device_id={"tp": frm}, device_id_type=MESH)
            wait(cp)
            return 0
        lax.fori_loop(0, n_dev - 1, body, 0)

    sems = (gssem, grsem)

    def blk(a, b, k, part=None):
        if part is None:
            return G.at[c, a, b, pl.ds(k * SUB, SUB)]
        return G.at[c, a, b, pl.ds(k * SUB + part * (SUB // 2), SUB // 2)]

    def line(b, k, a0=0, na=side):
        return G.at[c, pl.ds(a0, na), b, pl.ds(k * SUB, SUB)]

    def combine(b):
        heard(b, lambda cp: cp.wait_recv())
        st = ST[b]
        for h in range(CHUNK // 128):
            ms, ss, ws, ts = (st[:, 4 * h + q:4 * h + q + 1, :] for q in range(4))
            m = jnp.max(ms, axis=0)
            f = jnp.exp(ms - m[None])
            s = jnp.sum(ss * f, axis=0)
            w = jnp.sum(ws * f, axis=0)
            t = jnp.sum(ts, axis=0)
            ln = m + jnp.log(s)
            cols = pl.ds(b * CHUNK + h * 128, 128)
            out[0:1, cols] = ln
            out[1:2, cols] = ln - w / s
            out[2:3, cols] = t - ln
            LP[...] = LT[b, :, h * 128:(h + 1) * 128] - ln

            def turn(q, _, h=h):
                v = pl.ds(pl.multiple_of(q * 128, 128), 128)
                G[c, i, j, pl.ds(b * CHUNK + h * 128, 128), v] = bf16(LP[v].T)
                return 0
            lax.fori_loop(0, vpad // 128, turn, 0)
            for k in range((b * CHUNK + h * 128) // SUB, (b * CHUNK + (h + 1) * 128) // SUB):
                own = blk(i, j, k)
                start(remote(own, own, sems, 12 * k, R1))
                start(remote(own, own, sems, 12 * k + 1, L1))

    def first(k):
        left, right = prv(i), nxt(i)
        remote(blk(left, j, k), blk(left, j, k), sems, 12 * k, R1).wait_recv()
        b = blk(left, j, k, 0)
        start(remote(b, b, sems, 12 * k + 2, R1))
        remote(blk(right, j, k), blk(right, j, k), sems, 12 * k + 1, L1).wait_recv()
        b = blk(right, j, k, 1)
        start(remote(b, b, sems, 12 * k + 3, L1))

    def second(k):
        for part in range(2):
            b = blk(opp(i), j, k, part)
            remote(b, b, sems, 12 * k + 2 + part, R1).wait_recv()
        b = line(j, k)
        start(remote(b, b, sems, 12 * k + 4, R2))
        start(remote(b, b, sems, 12 * k + 5, L2))
        start(remote(b, b, sems, 12 * k + 8, PT))

    def third(k):
        b = line(prv(j), k)
        remote(b, b, sems, 12 * k + 4, R2).wait_recv()
        b2 = line(prv(j), k, 0, side // 2)
        start(remote(b2, b2, sems, 12 * k + 6, R2))
        start(remote(b, b, sems, 12 * k + 9, PT))
        b = line(nxt(j), k)
        remote(b, b, sems, 12 * k + 5, L2).wait_recv()
        b2 = line(nxt(j), k, side // 2, side // 2)
        start(remote(b2, b2, sems, 12 * k + 7, L2))
        start(remote(b, b, sems, 12 * k + 10, PT))

    def fourth(k):
        for part in range(2):
            b = line(opp(j), k, part * (side // 2), side // 2)
            remote(b, b, sems, 12 * k + 6 + part, R2).wait_recv()
        b = line(opp(j), k)
        start(remote(b, b, sems, 12 * k + 11, PT))

    def last(k):
        for q, g in enumerate((i, prv(i), nxt(i), opp(i))):
            b = G.at[1 - c, :, g, pl.ds(k * SUB, SUB)]
            remote(b, b, sems, 12 * k + 8 + q, PT).wait_recv()

    chains = []
    for b in range(chunks):
        loads["h%d" % b].wait()
        if b == 0:
            loads["wg"].wait()
            loads["wu"].wait()
        mlp(b)
        chains.append(chain(b))
        next(chains[b])
    loads["wv"].wait()
    for b in range(chunks):
        while True:
            stop = False
            for q in range(b, chunks):
                if next(chains[q], "end") == "end" and q == b:
                    stop = True
            if stop:
                break
        if b == 0:
            logits(0)
    for cp in sent:
        cp.wait_send()
    sent.clear()
    tell(0)
    for b in range(1, chunks):
        logits(b)
        tell(b)
    for b in range(chunks):
        combine(b)
    for k in range(subs + 4):
        for lag, act in ((0, first), (1, second), (2, third), (3, fourth), (4, last)):
            if 0 <= k - lag < subs:
                act(k - lag)
    for b in range(chunks):
        heard(b, lambda cp: cp.wait_send())
    for cp in sent:
        cp.wait_send()


def layout_kernel(side, v_loc, g, st, o, o0, o1, o2):
    r = pl.ds(pl.multiple_of(pl.program_id(0) * o.shape[0], o.shape[0]), o.shape[0])
    for fam in range(2):
        for a in range(side):
            for b in range(side):
                dev = ((b * side + a) * 2) if fam == 0 else ((a * side + b) * 2 + 1)
                o[:, dev * v_loc:(dev + 1) * v_loc] = g[fam, a, b, r, 0:v_loc]
    for q, one in enumerate((o0, o1, o2)):
        one[...] = st[q:q + 1]


def solution(mesh):
    n_dev = mesh.shape["tp"]
    side = math.isqrt(n_dev // 2)

    def device_step(hidden, w_gate, w_up, w_down, norm_gain, w_vocab, temperature, target):
        rows, d = hidden.shape
        f_loc, v_loc = w_gate.shape[1], w_vocab.shape[1]
        vpad = -(-v_loc // 128) * 128
        fpad = -(-f_loc // 128) * 128
        vm = pl.BlockSpec(memory_space=pltpu.VMEM)
        hbm = pl.BlockSpec(memory_space=pl.ANY)
        bf = jnp.bfloat16
        chunks, subs = rows // CHUNK, rows // SUB
        dma = pltpu.SemaphoreType.DMA
        g, stats = pl.pallas_call(
            functools.partial(tail_kernel, side, n_dev, f_loc, v_loc),
            out_shape=(pltpu.VMEM((2, side, side, rows, vpad), bf), pltpu.VMEM((8, rows), jnp.float32)),
            in_specs=[hbm, hbm, hbm, hbm, vm, hbm, vm, vm],
            out_specs=(vm, vm),
            scratch_shapes=[
                pltpu.VMEM((rows, d), bf),
                pltpu.VMEM((2 * fpad, d), bf),
                pltpu.VMEM((fpad, d), bf),
                pltpu.VMEM((rows, d), bf),
                pltpu.VMEM((vpad, d), bf),
                pltpu.VMEM((chunks, vpad, CHUNK), jnp.float32),
                pltpu.VMEM((vpad, 128), jnp.float32),
                pltpu.VMEM((chunks, n_dev, 8, 128), jnp.float32),
                dma((5 + chunks - 1,)),
                dma((24 * chunks,)), dma((24 * chunks,)),
                dma((12 * subs,)), dma((12 * subs,)),
                dma((chunks, n_dev - 1)), dma((chunks, n_dev - 1)),
            ],
            compiler_params=pltpu.CompilerParams(
                collective_id=0, has_side_effects=True, vmem_limit_bytes=30 << 20),
            name="tail",
        )(hidden, w_gate.T, w_up.T, w_down, norm_gain.reshape(1, d), w_vocab.T, temperature.reshape(1, rows),
          target.reshape(1, rows))

        step = 64
        one = jax.ShapeDtypeStruct((1, rows), jnp.float32)
        one_spec = pl.BlockSpec((1, rows), lambda s: (0, 0))
        log_probs, log_norm, entropy, target_logp = pl.pallas_call(
            functools.partial(layout_kernel, side, v_loc),
            out_shape=(jax.ShapeDtypeStruct((rows, n_dev * v_loc), bf), one, one, one),
            grid=(rows // step,),
            in_specs=[vm, vm],
            out_specs=(pl.BlockSpec((step, n_dev * v_loc), lambda s: (s, 0)), one_spec, one_spec, one_spec),
            compiler_params=pltpu.CompilerParams(vmem_limit_bytes=16 << 20),
            name="layout",
        )(g, stats)
        return log_norm.reshape(rows), entropy.reshape(rows), target_logp.reshape(rows), log_probs

    return jax.shard_map(
        device_step,
        mesh=mesh,
        in_specs=(P("dp", None), P(None, "tp"), P(None, "tp"), P("tp", None), P(None),
                  P(None, "tp"), P("dp"), P("dp")),
        out_specs=(P("dp"), P("dp"), P("dp"), P("dp", None)),
        check_vma=False,
    )
```

time: 385 us -> 205 us (0.53)
  waiting for transfers between devices: 209 us -> 0 us
  Pallas kernels: 0 us -> 182 us
  blocking collectives: 89.3 us -> 0 us
  matrix products: 21.7 us -> 0 us
  local copies, waits for them, and re-layouts: 41.9 us -> 21.6 us
  between operations: 14.1 us -> 0.65 us
  other arithmetic: 8.12 us -> 0 us
    pallas_call x0 -> x2, Pallas kernels: none -> 182 us  [the longest x1 169 us: device_step(): pl.pallas_call(functools.partial(tail_kernel, side, n_dev, f_loc, v_loc),...]
    psum x1 -> x0, waiting for transfers between devices: 105 us -> none  [device_step(): mlp_out = lax.psum(part_sum, 'tp')]
    all_gather x1 -> x0, waiting for transfers between devices: 104 us -> none  [device_step(): log_probs = lax.all_gather(local_probs, 'tp', axis=1, tiled=True)]
    pmax x1 -> x0, blocking collectives: 45.7 us -> none  [device_step(): row_max = lax.pmax(jnp.max(logits, axis=-1), 'tp')]
    psum x1 -> x0, blocking collectives: 43.6 us -> none  [device_step(): row_stats = lax.psum(local_stats, 'tp')]
    dot_general x3 -> x0, matrix products: 21.7 us -> none  [the longest x1 9.13 us: device_step(): jnp.dot(hidden_act, w_down, preferred_element_type=jnp.float32)]
    unnamed x17 -> x4, local copies, waits for them, and re-layouts: 41.9 us -> 21.6 us
    reduce_sum x2 -> x0, other arithmetic: 5.7 us -> none  [the longest x1 5.03 us: device_step(): jnp.mean(residual * residual, axis=-1, keepdims=True) + NORM_EPS]
  transfers between devices with their start and end apart: 2 -> 0, of which waited for: 2 -> 0; matrix products, arithmetic and copies ran while one was open for 0% -> 0% of each run, Pallas kernels for 0% -> 0%
where the time goes in v2:
time: 205 us
  Pallas kernels  182 us (89%)
  local copies, waits for them, and re-layouts  21.6 us (11%)
    pallas_call x1, Pallas kernels, device_step(): pl.pallas_call(functools.partial(tail_kernel, side, n_dev, f_loc, v_loc),...  169 us
    unnamed x4, local copies, waits for them, and re-layouts  21.6 us
    pallas_call x1, Pallas kernels, device_step(): pl.pallas_call(functools.partial(layout_kernel, side, v_loc), out_shape=(...  13.6 us

profile of v2, /device:TPU:97, one launch (start us, length us, event | category | flops | bytes accessed | tf_op | source)
XLA Modules:
  0.0 204.7 jit_solution(12453941271590855853)
XLA Ops:
  0.6 168.9 %tail.1 = (bf16[2,4,4,512,1024]{4,3,2,1,0:T(8,128)(2,1)S(1)}, f32[8,512]{1,0:T(8,128)S(1)}) custom-call(bf16[512,4096]{1,0:T(8,128)(2,1)} %h_hbm.1, bf16[344,4096]{1,0:T(8,128)(2,1)} %bitcast.10, bf16[344,4096]{1,0:T(8,128)(2,1)} %bitcast.11, bf16[344,4096]{1,0:T(8,128)(2,1)} %wd_hbm.1, f32[1,4096]{1,0:T(1,128)} %bitcast.12, bf16[1000,4096]{1,0:T(8,128)(2,1)} %bitcast.9, ...), custom_call_target="tpu_custom_call" | custom-call | tf_op jit(solution)/shard_map/tail/pallas_call | solution.py:396
  169.5 0.0 copy-start
  169.5 11.1 %copy-done = bf16[2,4,4,512,1024]{4,3,2,1,0:T(8,128)(2,1)} copy-done((bf16[2,4,4,512,1024]{4,3,2,1,0:T(8,128)(2,1)}, bf16[2,4,4,512,1024]{4,3,2,1,0:T(8,128)(2,1)S(1)}, u32[]{:S(2)}) %copy-start) | copy-done | bytes 33554456
  180.6 0.0 copy-start.1
  180.6 10.5 %copy-done.1 = bf16[2,4,4,512,1024]{4,3,2,1,0:T(8,128)(2,1)S(1)} copy-done((bf16[2,4,4,512,1024]{4,3,2,1,0:T(8,128)(2,1)S(1)}, bf16[2,4,4,512,1024]{4,3,2,1,0:T(8,128)(2,1)}, u32[]{:S(2)}) %copy-start.1) | copy-done | bytes 33554456
  191.1 13.6 %layout.1 = (bf16[512,32000]{1,0:T(8,128)(2,1)}, f32[1,512]{1,0:T(1,128)}, f32[1,512]{1,0:T(1,128)}, f32[1,512]{1,0:T(1,128)}) custom-call(bf16[2,4,4,512,1024]{4,3,2,1,0:T(8,128)(2,1)S(1)} %copy-done.1, f32[8,512]{1,0:T(8,128)S(1)} %get-tuple-element.11.st), custom_call_target="tpu_custom_call" | custom-call | tf_op jit(solution)/shard_map/layout/pallas_call | solution.py:424
Async XLA Ops:
  169.5 11.1 %copy-start = (bf16[2,4,4,512,1024]{4,3,2,1,0:T(8,128)(2,1)}, bf16[2,4,4,512,1024]{4,3,2,1,0:T(8,128)(2,1)S(1)}, u32[]{:S(2)}) copy-start(bf16[2,4,4,512,1024]{4,3,2,1,0:T(8,128)(2,1)S(1)} %get-tuple-element.10.g) | copy-start | bytes 100663296
  180.6 10.5 %copy-start.1 = (bf16[2,4,4,512,1024]{4,3,2,1,0:T(8,128)(2,1)S(1)}, bf16[2,4,4,512,1024]{4,3,2,1,0:T(8,128)(2,1)}, u32[]{:S(2)}) copy-start(bf16[2,4,4,512,1024]{4,3,2,1,0:T(8,128)(2,1)} %copy-done) | copy-start | bytes 100663296

commit v3 on v2

--- a/solution.py
+++ b/solution.py
@@ -41,7 +41,7 @@
 
 
 def tail_kernel(side, n_dev, f_loc, v_loc, h_hbm, wg_hbm, wu_hbm, wd_hbm, gain, wv_hbm, temp, target, G, out,
-                H, W, WD, X, WV, LT, LP, ST, lsem, ssem, rsem, gssem, grsem, stsem, strsem):
+                H, W, WD, X, WV, LT, ST, lsem, ssem, rsem, gssem, grsem, stsem, strsem):
     me, c, i, j, R1, L1, R2, L2, PT = place(side)
     rows, d = H.shape
     vpad = WV.shape[0]
@@ -52,7 +52,6 @@
     subs = rows // SUB
     n1 = CHUNK // 2
     n2 = n1 // side
-    n3 = n2 // side
     f32 = lambda v: v.astype(jnp.float32)
     bf16 = lambda v: v.astype(jnp.bfloat16)
     nxt = lambda v: lax.rem(v + 1, side)
@@ -86,11 +85,11 @@
     WD[f_loc:] = jnp.zeros((fpad - f_loc, d), WD.dtype)
     WV[v_loc:] = jnp.zeros((vpad - v_loc, d), WV.dtype)
 
-    sent = []
-
-    def start(cp):
+    sent, scratch_sent = [], []
+
+    def start(cp, scratch=False):
         cp.start()
-        sent.append(cp)
+        (scratch_sent if scratch else sent).append(cp)
         return cp
 
     Y = G.at[0, 0]
@@ -99,6 +98,7 @@
         gu = lax.dot_general(W[...], H[b * CHUNK:(b + 1) * CHUNK], NT, preferred_element_type=jnp.float32)
         g, u = gu[:fpad], gu[fpad:]
         a = bf16((g * lax.logistic(g) * u).T)
+        yield
         if b == 0:
             loads["wd"].wait()
             pl.semaphore_wait(barrier, n_dev - 1)
@@ -106,7 +106,7 @@
             Y[p, b * CHUNK:(b + 1) * CHUNK] = bf16(
                 jnp.dot(a, WD[:, p * PIECE:(p + 1) * PIECE], preferred_element_type=jnp.float32))
             theirs = Y.at[p, pl.ds(pl.multiple_of(b * CHUNK + (1 - c) * n1, n1), n1)]
-            start(remote(theirs, G.at[0, 1, p, pl.ds(b * n1, n1)], (ssem, rsem), 24 * b + p, PT))
+            start(remote(theirs, G.at[0, 1, p, pl.ds(b * n1, n1)], (ssem, rsem), 24 * b + p, PT), True)
 
     def chain(b):
         sems = (ssem, rsem)
@@ -115,7 +115,6 @@
         T = G.at[1, b]
         lo, hi, every = pl.ds(0, half), pl.ds(half, half), pl.ds(0, pieces)
         row1 = lambda g: pl.multiple_of(b * CHUNK + c * n1 + g * n2, n2)
-        row2 = lambda g: pl.multiple_of(b * CHUNK + c * n1 + i * n2 + g * n3, n3)
 
         def add_partner(g):
             at = pl.ds(row1(g), n2)
@@ -127,8 +126,8 @@
             ta, tl, tr = pl.ds(t0, n), pl.ds(t0 + n, n), pl.ds(t0 + 2 * n, n)
             prepare(opp(pos))
             far = pl.ds(row(opp(pos)), n)
-            m0 = start(remote(Y.at[lo, far], T.at[lo, ta], sems, k, R))
-            m1 = start(remote(Y.at[hi, far], T.at[hi, ta], sems, k + 1, L))
+            m0 = start(remote(Y.at[lo, far], T.at[lo, ta], sems, k, R), True)
+            m1 = start(remote(Y.at[hi, far], T.at[hi, ta], sems, k + 1, L), True)
             prepare(nxt(pos))
             prepare(prv(pos))
             right, left = pl.ds(row(nxt(pos)), n), pl.ds(row(prv(pos)), n)
@@ -136,11 +135,11 @@
             m0.wait_recv()
             for p in range(half):
                 Y[p, right] = bf16(f32(Y[p, right]) + f32(T[p, ta]))
-            m2 = start(remote(Y.at[every, right], T.at[every, tl], sems, k + 2, R))
+            m2 = start(remote(Y.at[every, right], T.at[every, tl], sems, k + 2, R), True)
             m1.wait_recv()
             for p in range(half, pieces):
                 Y[p, left] = bf16(f32(Y[p, left]) + f32(T[p, ta]))
-            m3 = start(remote(Y.at[every, left], T.at[every, tr], sems, k + 3, L))
+            m3 = start(remote(Y.at[every, left], T.at[every, tr], sems, k + 3, L), True)
             prepare(pos)
             yield
             m2.wait_recv()
@@ -162,22 +161,40 @@
             box = G.at[0, 1, p, pl.ds(b * n1, n1)]
             remote(box, box, sems, k0 + p, PT).wait_recv()
         own1 = pl.ds(row1(i), n2)
+        slot = lambda q: pl.ds(pl.multiple_of(side * n2 + q * n2, n2), n2)
 
         def keep1(p, total):
-            Y[p, own1] = bf16(total)
+            T[p, slot(j)] = bf16(total)
         yield from drive(ring_sum(i, row1, n2, R1, L1, 0, k0 + 4, add_partner), keep1)
+
+        mine, ahead, behind, across = (T.at[:, slot(q)] for q in (j, nxt(j), prv(j), opp(j)))
+        start(remote(mine, mine, sems, k0 + 8, R2), True)
+        start(remote(mine, mine, sems, k0 + 9, L2), True)
+        yield
+        remote(behind, behind, sems, k0 + 8, R2).wait_recv()
+        part = T.at[lo, slot(prv(j))]
+        start(remote(part, part, sems, k0 + 10, R2), True)
+        remote(ahead, ahead, sems, k0 + 9, L2).wait_recv()
+        part = T.at[hi, slot(nxt(j))]
+        start(remote(part, part, sems, k0 + 11, L2), True)
+        yield
+        for q, ps in ((10, lo), (11, hi)):
+            part = T.at[ps, slot(opp(j))]
+            remote(part, part, sems, k0 + q, R2).wait_recv()
         sums = []
-        yield from drive(ring_sum(j, row2, n3, R2, L2, 3 * n2, k0 + 8, lambda g: None), lambda p, t: sums.append(t))
-
-        mine = pl.ds(row2(j), n3)
-        square = jnp.zeros((n3, 1), jnp.float32)
+        square = jnp.zeros((n2, 1), jnp.float32)
         for p in range(pieces):
-            sums[p] = f32(H[mine, p * PIECE:(p + 1) * PIECE]) + sums[p]
-            square += jnp.sum(sums[p] * sums[p], axis=-1, keepdims=True)
+            y = f32(T[p, slot(0)])
+            for q in range(1, side):
+                y += f32(T[p, slot(q)])
+            r = f32(H[own1, p * PIECE:(p + 1) * PIECE]) + y
+            sums.append(r)
+            square += jnp.sum(r * r, axis=-1, keepdims=True)
         inv = lax.rsqrt(square / d + NORM_EPS)
         for p in range(pieces):
             cols = slice(p * PIECE, (p + 1) * PIECE)
-            X[mine, cols] = bf16(gain[0:1, cols] * sums[p] * inv)
+            X[own1, cols] = bf16(gain[0:1, cols] * sums[p] * inv)
+        passed.add(b)
 
         left_half, right_half = pl.ds(0, d // 2), pl.ds(d // 2, d // 2)
 
@@ -199,9 +216,6 @@
             remote(at(far, right_half), at(far, right_half), sems, k + 3, L).wait_recv()
             yield far
 
-        for got in ring_gather(j, row2, n3, R2, L2, k0 + 12):
-            if got is None:
-                yield
         k = k0 + 20
         for got in ring_gather(i, row1, n2, R1, L1, k0 + 16):
             if got is None:
@@ -275,11 +289,10 @@
             out[0:1, cols] = ln
             out[1:2, cols] = ln - w / s
             out[2:3, cols] = t - ln
-            LP[...] = LT[b, :, h * 128:(h + 1) * 128] - ln
-
-            def turn(q, _, h=h):
+
+            def turn(q, _, h=h, ln=ln):
                 v = pl.ds(pl.multiple_of(q * 128, 128), 128)
-                G[c, i, j, pl.ds(b * CHUNK + h * 128, 128), v] = bf16(LP[v].T)
+                G[c, i, j, pl.ds(b * CHUNK + h * 128, 128), v] = bf16((LT[b, v, h * 128:(h + 1) * 128] - ln).T)
                 return 0
             lax.fori_loop(0, vpad // 128, turn, 0)
             for k in range((b * CHUNK + h * 128) // SUB, (b * CHUNK + (h + 1) * 128) // SUB):
@@ -329,54 +342,75 @@
             b = G.at[1 - c, :, g, pl.ds(k * SUB, SUB)]
             remote(b, b, sems, 12 * k + 8 + q, PT).wait_recv()
 
-    chains = []
-    for b in range(chunks):
+    passed = set()
+    loads["h0"].wait()
+    loads["wg"].wait()
+    loads["wu"].wait()
+    for _ in mlp(0):
+        pass
+    chains = [chain(b) for b in range(chunks)]
+    next(chains[0])
+    next(chains[0])
+    for b in range(1, chunks):
         loads["h%d" % b].wait()
-        if b == 0:
-            loads["wg"].wait()
-            loads["wu"].wait()
-        mlp(b)
-        chains.append(chain(b))
+        for _ in mlp(b):
+            next(chains[0])
         next(chains[b])
     loads["wv"].wait()
-    for b in range(chunks):
-        while True:
-            stop = False
-            for q in range(b, chunks):
-                if next(chains[q], "end") == "end" and q == b:
-                    stop = True
-            if stop:
-                break
-        if b == 0:
-            logits(0)
-    for cp in sent:
+    while next(chains[0], "end") != "end":
+        for b in range(1, chunks):
+            next(chains[b], None)
+    logits(0)
+    assert len(passed) == chunks
+    for cp in scratch_sent:
         cp.wait_send()
-    sent.clear()
     tell(0)
+    for b in range(1, chunks):
+        for _ in chains[b]:
+            pass
+    combine(0)
     for b in range(1, chunks):
         logits(b)
         tell(b)
-    for b in range(chunks):
-        combine(b)
-    for k in range(subs + 4):
-        for lag, act in ((0, first), (1, second), (2, third), (3, fourth), (4, last)):
-            if 0 <= k - lag < subs:
-                act(k - lag)
+    per = CHUNK // SUB
+    events = [(k + lag, lag, act, k) for k in range(subs)
+              for lag, act in ((0, first), (1, second), (2, third), (3, fourth), (4, last))]
+    done = 1
+    for when, lag, act, k in sorted(events, key=lambda e: (e[0], e[1])):
+        if lag == 0 and k == done * per:
+            combine(done)
+            done += 1
+        act(k)
     for b in range(chunks):
         heard(b, lambda cp: cp.wait_send())
     for cp in sent:
         cp.wait_send()
 
 
-def layout_kernel(side, v_loc, g, st, o, o0, o1, o2):
-    r = pl.ds(pl.multiple_of(pl.program_id(0) * o.shape[0], o.shape[0]), o.shape[0])
-    for fam in range(2):
-        for a in range(side):
-            for b in range(side):
-                dev = ((b * side + a) * 2) if fam == 0 else ((a * side + b) * 2 + 1)
-                o[:, dev * v_loc:(dev + 1) * v_loc] = g[fam, a, b, r, 0:v_loc]
-    for q, one in enumerate((o0, o1, o2)):
-        one[...] = st[q:q + 1]
+def layout_kernel(side, v_loc, g, o, stage, sem):
+    slots, step, _ = stage.shape
+    steps = o.shape[0] // step
+
+    def out(s, slot):
+        return pltpu.make_async_copy(stage.at[slot], o.at[pl.ds(pl.multiple_of(s * step, step), step)], sem.at[slot])
+
+    def body(s, _):
+        slot = lax.rem(s, slots)
+
+        @pl.when(s >= slots)
+        def _():
+            out(s - slots, slot).wait()
+        r = pl.ds(pl.multiple_of(s * step, step), step)
+        for fam in range(2):
+            for a in range(side):
+                for b in range(side):
+                    dev = ((b * side + a) * 2) if fam == 0 else ((a * side + b) * 2 + 1)
+                    stage[slot, :, dev * v_loc:(dev + 1) * v_loc] = g[fam, a, b, r, 0:v_loc]
+        out(s, slot).start()
+        return 0
+    lax.fori_loop(0, steps, body, 0)
+    for s in range(steps - slots, steps):
+        out(s, s % slots).wait()
 
 
 def solution(mesh):
@@ -405,7 +439,6 @@
                 pltpu.VMEM((rows, d), bf),
                 pltpu.VMEM((vpad, d), bf),
                 pltpu.VMEM((chunks, vpad, CHUNK), jnp.float32),
-                pltpu.VMEM((vpad, 128), jnp.float32),
                 pltpu.VMEM((chunks, n_dev, 8, 128), jnp.float32),
                 dma((5 + chunks - 1,)),
                 dma((24 * chunks,)), dma((24 * chunks,)),
@@ -418,19 +451,16 @@
         )(hidden, w_gate.T, w_up.T, w_down, norm_gain.reshape(1, d), w_vocab.T, temperature.reshape(1, rows),
           target.reshape(1, rows))
 
-        step = 64
-        one = jax.ShapeDtypeStruct((1, rows), jnp.float32)
-        one_spec = pl.BlockSpec((1, rows), lambda s: (0, 0))
-        log_probs, log_norm, entropy, target_logp = pl.pallas_call(
+        log_probs = pl.pallas_call(
             functools.partial(layout_kernel, side, v_loc),
-            out_shape=(jax.ShapeDtypeStruct((rows, n_dev * v_loc), bf), one, one, one),
-            grid=(rows // step,),
-            in_specs=[vm, vm],
-            out_specs=(pl.BlockSpec((step, n_dev * v_loc), lambda s: (s, 0)), one_spec, one_spec, one_spec),
+            out_shape=jax.ShapeDtypeStruct((rows, n_dev * v_loc), bf),
+            in_specs=[vm],
+            out_specs=hbm,
+            scratch_shapes=[pltpu.VMEM((4, 16, n_dev * v_loc), bf), dma((4,))],
             compiler_params=pltpu.CompilerParams(vmem_limit_bytes=16 << 20),
             name="layout",
-        )(g, stats)
-        return log_norm.reshape(rows), entropy.reshape(rows), target_logp.reshape(rows), log_probs
+        )(g)
+        return stats[0], stats[1], stats[2], log_probs
 
     return jax.shard_map(
         device_step,

time: 205 us -> 175 us (0.85)
  local copies, waits for them, and re-layouts: 21.6 us -> 0.59 us
  Pallas kernels: 182 us -> 174 us
    unnamed x4 -> x0, local copies, waits for them, and re-layouts: 21.6 us -> none
    pallas_call x1, Pallas kernels: 169 us -> 162 us  [device_step(): pl.pallas_call(functools.partial(tail_kernel, side, n_dev, f_loc, v_loc),...]
    pallas_call x1, Pallas kernels: 13.6 us -> 11.4 us  [device_step(): pl.pallas_call(functools.partial(layout_kernel, side, v_loc), out_shape=j...]
where the time goes in v3:
time: 175 us
  Pallas kernels  174 us (99%)
    pallas_call x1, Pallas kernels, device_step(): pl.pallas_call(functools.partial(tail_kernel, side, n_dev, f_loc, v_loc),...  162 us
    pallas_call x1, Pallas kernels, device_step(): pl.pallas_call(functools.partial(layout_kernel, side, v_loc), out_shape=j...  11.4 us

profile of v3, /device:TPU:97, one launch (start us, length us, event | category | flops | bytes accessed | tf_op | source)
XLA Modules:
  0.0 175.1 jit_solution(1236510259818494294)
XLA Ops:
  0.6 162.3 %tail.1 = (bf16[2,4,4,512,1024]{4,3,2,1,0:T(8,128)(2,1)S(1)}, f32[8,512]{1,0:T(8,128)S(1)}) custom-call(bf16[512,4096]{1,0:T(8,128)(2,1)} %h_hbm.1, bf16[344,4096]{1,0:T(8,128)(2,1)} %bitcast.10, bf16[344,4096]{1,0:T(8,128)(2,1)} %bitcast.11, bf16[344,4096]{1,0:T(8,128)(2,1)} %wd_hbm.1, f32[1,4096]{1,0:T(1,128)} %bitcast.12, bf16[1000,4096]{1,0:T(8,128)(2,1)} %bitcast.9, ...), custom_call_target="tpu_custom_call" | custom-call | tf_op jit(solution)/shard_map/tail/pallas_call | solution.py:430
  163.0 0.6 fusion
  163.6 11.4 %layout.1 = bf16[512,32000]{1,0:T(8,128)(2,1)} custom-call(bf16[2,4,4,512,1024]{4,3,2,1,0:T(8,128)(2,1)S(1)} %get-tuple-element.7.g), custom_call_target="tpu_custom_call" | custom-call | tf_op jit(solution)/shard_map/layout/pallas_call | solution.py:454

commit v4 on v3

v4 whole, which is shorter than its diff:
```python
import functools
import math

import jax
import jax.numpy as jnp
from jax import lax
from jax.experimental import pallas as pl
from jax.experimental.pallas import tpu as pltpu
from jax.sharding import PartitionSpec as P

NORM_EPS = 1e-6
MESH = pl.DeviceIdType.MESH
NT = (((1,), (1,)), ((), ()))
PIECE = 1024
CHUNK = 128
GROUP = 256
LAG = 1

def place(side):
    me = lax.axis_index("tp")
    c = lax.rem(me, 2)
    chip = lax.div(me, 2)
    x, y = lax.rem(chip, side), lax.div(chip, side)
    i = x * (1 - c) + y * c
    j = y * (1 - c) + x * c
    s1 = 2 + (2 * side - 2) * c
    s2 = 2 * side - (2 * side - 2) * c

    def dev(a, b):
        return a * s1 + b * s2 + c

    nxt = lambda v: lax.rem(v + 1, side)
    prv = lambda v: lax.rem(v + side - 1, side)
    return me, c, i, j, dev(nxt(i), j), dev(prv(i), j), dev(i, nxt(j)), dev(i, prv(j)), me + 1 - 2 * c


def remote(src, dst, sems, k, to):
    return pltpu.make_async_remote_copy(
        src_ref=src, dst_ref=dst, send_sem=sems[0].at[k], recv_sem=sems[1].at[k],
        device_id={"tp": to}, device_id_type=MESH)


def tail_kernel(side, n_dev, f_loc, v_loc, h_hbm, wg_hbm, wu_hbm, wd_hbm, gain, wv_hbm, temp, target, G, out,
                H, W, WD, X, WV, LT, ST, lsem, ssem, rsem, gssem, grsem, stsem, strsem):
    me, c, i, j, R1, L1, R2, L2, PT = place(side)
    rows, d = H.shape
    vpad = WV.shape[0]
    fpad = WD.shape[0]
    pieces = d // PIECE
    half = pieces // 2
    chunks = rows // CHUNK
    groups = rows // GROUP
    per = GROUP // CHUNK
    n1 = CHUNK // 2
    n2 = n1 // side
    f32 = lambda v: v.astype(jnp.float32)
    bf16 = lambda v: v.astype(jnp.bfloat16)
    nxt = lambda v: lax.rem(v + 1, side)
    prv = lambda v: lax.rem(v + side - 1, side)
    opp = lambda v: lax.rem(v + 2, side)

    loads = {}

    def load(name, src, dst):
        cp = pltpu.make_async_copy(src, dst, lsem.at[len(loads)])
        cp.start()
        loads[name] = cp

    for p in range(pieces):
        cols = pl.ds(p * PIECE, PIECE)
        load(("h", p), h_hbm.at[pl.ds(0, GROUP), cols], H.at[pl.ds(0, GROUP), cols])
        load(("g", p), wg_hbm.at[:, cols], W.at[pl.ds(0, f_loc), cols])
        load(("u", p), wu_hbm.at[:, cols], W.at[pl.ds(fpad, f_loc), cols])

    barrier = pltpu.get_barrier_semaphore()

    def greet(t, _):
        to = lax.rem(me + 1 + t, n_dev)
        pl.semaphore_signal(barrier, inc=1, device_id={"tp": to}, device_id_type=MESH)
        return 0
    lax.fori_loop(0, n_dev - 1, greet, 0)
    W[f_loc:fpad] = jnp.zeros((fpad - f_loc, d), W.dtype)
    W[fpad + f_loc:] = jnp.zeros((fpad - f_loc, d), W.dtype)
    WD[f_loc:] = jnp.zeros((fpad - f_loc, d), WD.dtype)
    WV[v_loc:] = jnp.zeros((vpad - v_loc, d), WV.dtype)

    sent, scratch_sent = [], [[] for _ in range(chunks)]

    def start(cp, scratch=None):
        cp.start()
        (sent if scratch is None else scratch_sent[scratch]).append(cp)
        return cp

    Y = G.at[0, 0]

    def mlp(b):
        cut = slice(b * GROUP, (b + 1) * GROUP)
        if b == 0:
            gu = None
            for p in range(pieces):
                for name in ("h", "g", "u"):
                    loads[name, p].wait()
                if p == pieces - 1:
                    load("wd", wd_hbm, WD.at[pl.ds(0, f_loc)])
                cols = slice(p * PIECE, (p + 1) * PIECE)
                more = lax.dot_general(W[:, cols], H[cut, cols], NT, preferred_element_type=jnp.float32)
                gu = more if gu is None else gu + more
            for q in range(1, rows // GROUP):
                load("h%d" % q, h_hbm.at[pl.ds(q * GROUP, GROUP)], H.at[pl.ds(q * GROUP, GROUP)])
            load("wv", wv_hbm, WV.at[pl.ds(0, v_loc)])
        else:
            loads["h%d" % b].wait()
            gu = lax.dot_general(W[...], H[cut], NT, preferred_element_type=jnp.float32)
        g, u = gu[:fpad], gu[fpad:]
        a = bf16((g * lax.logistic(g) * u).T)
        yield
        if b == 0:
            loads["wd"].wait()
            pl.semaphore_wait(barrier, n_dev - 1)
        for p in range(pieces):
            Y[p, cut] = bf16(
                jnp.dot(a, WD[:, p * PIECE:(p + 1) * PIECE], preferred_element_type=jnp.float32))
            for q in range(b * GROUP // CHUNK, (b + 1) * GROUP // CHUNK):
                theirs = Y.at[p, pl.ds(pl.multiple_of(q * CHUNK + (1 - c) * n1, n1), n1)]
                start(remote(theirs, G.at[0, 1, p, pl.ds(q * CHUNK, n1)], (ssem, rsem), 26 * q + p, PT), q)

    def chain(b):
        sems = (ssem, rsem)
        k0 = 26 * b
        P0 = G.at[0, 1]
        T = G.at[1, 0]
        lo, hi, every = pl.ds(0, half), pl.ds(half, half), pl.ds(0, pieces)
        row1 = lambda g: pl.multiple_of(b * CHUNK + c * n1 + g * n2, n2)

        def add_partner(g):
            at = pl.ds(row1(g), n2)
            frm = pl.ds(pl.multiple_of(b * CHUNK + g * n2, n2), n2)
            for p in range(pieces):
                Y[p, at] = bf16(f32(Y[p, at]) + f32(P0[p, frm]))

        def ring_sum(pos, row, n, R, L, t0, k, prepare):
            ta, tl, tr = pl.ds(t0, n), pl.ds(t0 + n, n), pl.ds(t0 + 2 * n, n)
            prepare(opp(pos))
            far = pl.ds(row(opp(pos)), n)
            right, left = pl.ds(row(nxt(pos)), n), pl.ds(row(prv(pos)), n)
            m0 = start(remote(Y.at[lo, far], T.at[lo, ta], sems, k, R), b)
            m1 = start(remote(Y.at[hi, far], T.at[hi, ta], sems, k + 1, L), b)
            prepare(nxt(pos))
            m2 = start(remote(Y.at[hi, right], T.at[hi, tl], sems, k + 2, R), b)
            prepare(prv(pos))
            m3 = start(remote(Y.at[lo, left], T.at[lo, tr], sems, k + 3, L), b)
            yield
            m0.wait_recv()
            for p in range(half):
                Y[p, right] = bf16(f32(Y[p, right]) + f32(T[p, ta]))
            m4 = start(remote(Y.at[lo, right], T.at[lo, tl], sems, k + 4, R), b)
            m1.wait_recv()
            for p in range(half, pieces):
                Y[p, left] = bf16(f32(Y[p, left]) + f32(T[p, ta]))
            m5 = start(remote(Y.at[hi, left], T.at[hi, tr], sems, k + 5, L), b)
            prepare(pos)
            yield
            for m in (m2, m3, m4, m5):
                m.wait_recv()
            own = pl.ds(row(pos), n)
            for p in range(pieces):
                total = f32(Y[p, own]) + f32(T[p, tl]) + f32(T[p, tr])
                yield p, total

        def drive(steps, keep):
            for got in steps:
                if got is None:
                    yield
                else:
                    keep(*got)

        yield
        for p in range(pieces):
            box = G.at[0, 1, p, pl.ds(b * CHUNK, n1)]
            remote(box, box, sems, k0 + p, PT).wait_recv()
        own1 = pl.ds(row1(i), n2)
        slot = lambda q: pl.ds(pl.multiple_of(b * CHUNK + side * n2 + q * n2, n2), n2)

        def keep1(p, total):
            T[p, slot(j)] = bf16(total)
        yield from drive(ring_sum(i, row1, n2, R1, L1, b * CHUNK, k0 + 4, add_partner), keep1)

        at = lambda ps, q: T.at[ps, slot(q)]
        for q, (ps, to) in enumerate(((lo, R2), (hi, L2), (hi, R2), (lo, L2))):
            start(remote(at(ps, j), at(ps, j), sems, k0 + 10 + q, to), b)
        yield
        remote(at(lo, prv(j)), at(lo, prv(j)), sems, k0 + 10, R2).wait_recv()
        start(remote(at(lo, prv(j)), at(lo, prv(j)), sems, k0 + 14, R2), b)
        remote(at(hi, nxt(j)), at(hi, nxt(j)), sems, k0 + 11, L2).wait_recv()
        start(remote(at(hi, nxt(j)), at(hi, nxt(j)), sems, k0 + 15, L2), b)
        yield
        for q, ps, frm in ((12, hi, prv(j)), (13, lo, nxt(j)), (14, lo, opp(j)), (15, hi, opp(j))):
            remote(at(ps, frm), at(ps, frm), sems, k0 + q, R2).wait_recv()
        sums = []
        square = jnp.zeros((n2, 1), jnp.float32)
        for p in range(pieces):
            y = f32(T[p, slot(0)])
            for q in range(1, side):
                y += f32(T[p, slot(q)])
            r = f32(H[own1, p * PIECE:(p + 1) * PIECE]) + y
            sums.append(r)
            square += jnp.sum(r * r, axis=-1, keepdims=True)
        inv = lax.rsqrt(square / d + NORM_EPS)
        for p in range(pieces):
            cols = slice(p * PIECE, (p + 1) * PIECE)
            X[own1, cols] = bf16(gain[0:1, cols] * sums[p] * inv)

        left_half, right_half = pl.ds(0, d // 2), pl.ds(d // 2, d // 2)

        at = lambda g, cols=pl.ds(0, d): X.at[pl.ds(row1(g), n2), cols]
        for q, (cols, to) in enumerate(((left_half, R1), (right_half, L1), (right_half, R1), (left_half, L1))):
            start(remote(at(i, cols), at(i, cols), sems, k0 + 16 + q, to))
        start(remote(at(i), at(i), sems, k0 + 22, PT))
        yield
        left, right, far = prv(i), nxt(i), opp(i)
        remote(at(left, left_half), at(left, left_half), sems, k0 + 16, R1).wait_recv()
        start(remote(at(left, left_half), at(left, left_half), sems, k0 + 20, R1))
        remote(at(right, right_half), at(right, right_half), sems, k0 + 17, L1).wait_recv()
        start(remote(at(right, right_half), at(right, right_half), sems, k0 + 21, L1))
        remote(at(left, right_half), at(left, right_half), sems, k0 + 18, R1).wait_recv()
        start(remote(at(left), at(left), sems, k0 + 23, PT))
        remote(at(right, left_half), at(right, left_half), sems, k0 + 19, L1).wait_recv()
        start(remote(at(right), at(right), sems, k0 + 24, PT))
        yield
        remote(at(far, left_half), at(far, left_half), sems, k0 + 20, R1).wait_recv()
        remote(at(far, right_half), at(far, right_half), sems, k0 + 21, L1).wait_recv()
        start(remote(at(far), at(far), sems, k0 + 25, PT))
        yield
        for q, g in enumerate((j, prv(j), nxt(j), opp(j))):
            line = X.at[pl.ds(pl.multiple_of(b * CHUNK + (1 - c) * n1 + g * n2, n2), n2)]
            remote(line, line, sems, k0 + 22 + q, PT).wait_recv()

    vid = lax.broadcasted_iota(jnp.int32, (vpad, GROUP), 0)

    def logits(b):
        cols = slice(b * GROUP, (b + 1) * GROUP)
        l = lax.dot_general(WV[...], X[cols], NT, preferred_element_type=jnp.float32) / temp[0:1, cols]
        LT[b] = l
        real = vid < v_loc
        m = jnp.max(jnp.where(real, l, -jnp.inf), axis=0, keepdims=True)
        e = jnp.where(real, jnp.exp(l - m), 0.0)
        s = jnp.sum(e, axis=0, keepdims=True)
        w = jnp.sum(e * l, axis=0, keepdims=True)
        ids = target[0:1, cols] - me * v_loc
        t = jnp.sum(jnp.where((vid == ids) & real, l, 0.0), axis=0, keepdims=True)
        both = [v[:, h * CHUNK:(h + 1) * CHUNK] for h in range(per) for v in (m, s, w, t)]
        ST[b, me] = jnp.concatenate(both, axis=0)
        for q in range(b * per, (b + 1) * per):
            for cp in scratch_sent[q]:
                cp.wait_send()
        tell(b)

    def tell(b):
        def body(t, _):
            to = lax.rem(me + 1 + t, n_dev)
            pltpu.make_async_remote_copy(
                src_ref=ST.at[b, me], dst_ref=ST.at[b, me], send_sem=stsem.at[b, t], recv_sem=strsem.at[b, t],
                device_id={"tp": to}, device_id_type=MESH).start()
            return 0
        lax.fori_loop(0, n_dev - 1, body, 0)

    def heard(b, wait):
        def body(t, _):
            frm = lax.rem(me + n_dev - 1 - t, n_dev)
            cp = pltpu.make_async_remote_copy(
                src_ref=ST.at[b, me], dst_ref=ST.at[b, frm], send_sem=stsem.at[b, t], recv_sem=strsem.at[b, t],
                device_id={"tp": frm}, device_id_type=MESH)
            wait(cp)
            return 0
        lax.fori_loop(0, n_dev - 1, body, 0)

    sems = (gssem, grsem)

    def blk(a, k, part):
        return G.at[c, a, j, pl.ds(k * CHUNK + part * (CHUNK // 2), CHUNK // 2)]

    def line(b, k):
        return G.at[c, :, b, pl.ds(k * CHUNK, CHUNK)]

    def one_of(a, b, k):
        return G.at[c, a, b, pl.ds(k * CHUNK, CHUNK)]

    def move(ref, k, q, to):
        start(remote(ref, ref, sems, 22 * k + q, to))

    def got(ref, k, q):
        remote(ref, ref, sems, 22 * k + q, PT).wait_recv()

    def combine(b):
        group, part = b // per, b % per
        if part == 0:
            heard(group, lambda cp: cp.wait_recv())
        st = ST[group]
        ms, ss, ws, ts = (st[:, q:q + 1, :] for q in range(4 * part, 4 * part + 4))
        m = jnp.max(ms, axis=0)
        f = jnp.exp(ms - m[None])
        s = jnp.sum(ss * f, axis=0)
        w = jnp.sum(ws * f, axis=0)
        t = jnp.sum(ts, axis=0)
        ln = m + jnp.log(s)
        cols = pl.ds(b * CHUNK, CHUNK)
        out[0:1, cols] = ln
        out[1:2, cols] = ln - w / s
        out[2:3, cols] = t - ln

        def turn(q, _):
            v = pl.ds(pl.multiple_of(q * 128, 128), 128)
            G[c, i, j, cols, v] = bf16((LT[group, v, part * CHUNK:(part + 1) * CHUNK] - ln).T)
            return 0
        lax.fori_loop(0, vpad // 128, turn, 0)
        for q, (bit, to) in enumerate(((0, R1), (1, L1), (1, R1), (0, L1))):
            move(blk(i, b, bit), b, q, to)

    def first(k):
        left, right = prv(i), nxt(i)
        got(blk(left, k, 0), k, 0)
        move(blk(left, k, 0), k, 4, R1)
        got(blk(right, k, 1), k, 1)
        move(blk(right, k, 1), k, 5, L1)

    def second(k):
        got(blk(prv(i), k, 1), k, 2)
        got(blk(nxt(i), k, 0), k, 3)
        got(blk(opp(i), k, 0), k, 4)
        got(blk(opp(i), k, 1), k, 5)
        move(line(j, k), k, 18, PT)

    toR = tuple(range(side))
    toL = toR[side // 2:] + toR[:side // 2]

    def send(k, q):
        move(one_of(toR[q], j, k), k, 6 + q, R2)
        move(one_of(toL[q], j, k), k, 6 + side + q, L2)

    def third(k):
        for q in range(side // 2):
            b = one_of(toR[q], prv(j), k)
            got(b, k, 6 + q)
            move(b, k, 6 + 2 * side + q, R2)
            b = one_of(toL[q], nxt(j), k)
            got(b, k, 6 + side + q)
            move(b, k, 6 + 2 * side + side // 2 + q, L2)

    def fourth(k):
        for q in range(side // 2, side):
            got(one_of(toR[q], prv(j), k), k, 6 + q)
        move(line(prv(j), k), k, 19, PT)
        for q in range(side // 2, side):
            got(one_of(toL[q], nxt(j), k), k, 6 + side + q)
        move(line(nxt(j), k), k, 20, PT)
        for q in range(side // 2):
            got(one_of(toR[q], opp(j), k), k, 6 + 2 * side + q)
            got(one_of(toL[q], opp(j), k), k, 6 + 2 * side + side // 2 + q)
        move(line(opp(j), k), k, 21, PT)

    def last(k):
        for q, g in enumerate((i, prv(i), nxt(i), opp(i))):
            got(G.at[1 - c, :, g, pl.ds(k * CHUNK, CHUNK)], k, 18 + q)

    def lockstep(g):
        mine = [chain(b) for b in range(g * per, (g + 1) * per)]
        for one in mine:
            next(one)
        ended = False
        while not ended:
            for one in mine:
                ended = next(one, "end") == "end"
            if not ended:
                yield

    assert groups == 2 and per == 2
    for _ in mlp(0):
        pass
    one, two = lockstep(0), lockstep(1)
    next(one)
    for _ in mlp(1):
        next(one)
    loads["wv"].wait()
    rnd = 0
    while next(one, "end") != "end":
        rnd += 1
        if rnd > LAG:
            next(two)
    def both(k):
        second(k)
        for q in range(side):
            send(k, q)

    logits(0)
    next(two)
    combine(0)
    combine(1)
    next(two, None)
    first(0)
    next(two, None)
    second(0)
    send(0, 0)
    first(1)
    next(two, None)
    send(0, 1)
    for _ in two:
        pass
    send(0, 2)
    logits(1)
    send(0, 3)
    third(0)
    both(1)
    combine(2)
    combine(3)
    for act, k in ((first, 2), (third, 1), (first, 3), (fourth, 0), (both, 2), (fourth, 1), (both, 3), (last, 0),
                   (third, 2), (last, 1), (third, 3), (fourth, 2), (last, 2), (fourth, 3), (last, 3)):
        act(k)
    for b in range(groups):
        heard(b, lambda cp: cp.wait_send())
    for cp in sent:
        cp.wait_send()


def layout_kernel(side, v_loc, g, o, stage, sem):
    slots, step, _ = stage.shape
    steps = o.shape[0] // step

    def out(s, slot):
        return pltpu.make_async_copy(stage.at[slot], o.at[pl.ds(pl.multiple_of(s * step, step), step)], sem.at[slot])

    def body(s, _):
        slot = lax.rem(s, slots)

        @pl.when(s >= slots)
        def _():
            out(s - slots, slot).wait()
        r = pl.ds(pl.multiple_of(s * step, step), step)
        for fam in range(2):
            for a in range(side):
                for b in range(side):
                    dev = ((b * side + a) * 2) if fam == 0 else ((a * side + b) * 2 + 1)
                    stage[slot, :, dev * v_loc:(dev + 1) * v_loc] = g[fam, a, b, r, 0:v_loc]
        out(s, slot).start()
        return 0
    lax.fori_loop(0, steps, body, 0)
    for s in range(steps - slots, steps):
        out(s, s % slots).wait()


def solution(mesh):
    n_dev = mesh.shape["tp"]
    side = math.isqrt(n_dev // 2)

    def device_step(hidden, w_gate, w_up, w_down, norm_gain, w_vocab, temperature, target):
        rows, d = hidden.shape
        f_loc, v_loc = w_gate.shape[1], w_vocab.shape[1]
        vpad = -(-v_loc // 128) * 128
        fpad = -(-f_loc // 128) * 128
        vm = pl.BlockSpec(memory_space=pltpu.VMEM)
        hbm = pl.BlockSpec(memory_space=pl.ANY)
        bf = jnp.bfloat16
        chunks, groups = rows // CHUNK, rows // GROUP
        dma = pltpu.SemaphoreType.DMA
        g, stats = pl.pallas_call(
            functools.partial(tail_kernel, side, n_dev, f_loc, v_loc),
            out_shape=(pltpu.VMEM((2, side, side, rows, vpad), bf), pltpu.VMEM((8, rows), jnp.float32)),
            in_specs=[hbm, hbm, hbm, hbm, vm, hbm, vm, vm],
            out_specs=(vm, vm),
            scratch_shapes=[
                pltpu.VMEM((rows, d), bf),
                pltpu.VMEM((2 * fpad, d), bf),
                pltpu.VMEM((fpad, d), bf),
                pltpu.VMEM((rows, d), bf),
                pltpu.VMEM((vpad, d), bf),
                pltpu.VMEM((groups, vpad, GROUP), jnp.float32),
                pltpu.VMEM((groups, n_dev, 8, CHUNK), jnp.float32),
                dma((3 * (d // PIECE) + groups + 1,)),
                dma((26 * chunks,)), dma((26 * chunks,)),
                dma((22 * chunks,)), dma((22 * chunks,)),
                dma((groups, n_dev - 1)), dma((groups, n_dev - 1)),
            ],
            compiler_params=pltpu.CompilerParams(
                collective_id=0, has_side_effects=True, vmem_limit_bytes=30 << 20),
            name="tail",
        )(hidden, w_gate.T, w_up.T, w_down, norm_gain.reshape(1, d), w_vocab.T, temperature.reshape(1, rows),
          target.reshape(1, rows))

        log_probs = pl.pallas_call(
            functools.partial(layout_kernel, side, v_loc),
            out_shape=jax.ShapeDtypeStruct((rows, n_dev * v_loc), bf),
            in_specs=[vm],
            out_specs=hbm,
            scratch_shapes=[pltpu.VMEM((4, 16, n_dev * v_loc), bf), dma((4,))],
            compiler_params=pltpu.CompilerParams(vmem_limit_bytes=16 << 20),
            name="layout",
        )(g)
        return stats[0], stats[1], stats[2], log_probs

    return jax.shard_map(
        device_step,
        mesh=mesh,
        in_specs=(P("dp", None), P(None, "tp"), P(None, "tp"), P("tp", None), P(None),
                  P(None, "tp"), P("dp"), P("dp")),
        out_specs=(P("dp"), P("dp"), P("dp"), P("dp", None)),
        check_vma=False,
    )
```

time: 175 us -> 169 us (0.966)
  Pallas kernels: 174 us -> 167 us
    pallas_call x1, Pallas kernels: 162 us -> 156 us  [device_step(): pl.pallas_call(functools.partial(tail_kernel, side, n_dev, f_loc, v_loc),...]
where the time goes in v4:
time: 169 us
  Pallas kernels  167 us (99%)
    pallas_call x1, Pallas kernels, device_step(): pl.pallas_call(functools.partial(tail_kernel, side, n_dev, f_loc, v_loc),...  156 us
    pallas_call x1, Pallas kernels, device_step(): pl.pallas_call(functools.partial(layout_kernel, side, v_loc), out_shape=j...  11.4 us

profile of v4, /device:TPU:97, one launch (start us, length us, event | category | flops | bytes accessed | tf_op | source)
XLA Modules:
  0.0 168.9 jit_solution(8026803579246351029)
XLA Ops:
  0.6 156.1 %tail.1 = (bf16[2,4,4,512,1024]{4,3,2,1,0:T(8,128)(2,1)S(1)}, f32[8,512]{1,0:T(8,128)S(1)}) custom-call(bf16[512,4096]{1,0:T(8,128)(2,1)} %h_hbm.1, bf16[344,4096]{1,0:T(8,128)(2,1)} %bitcast.10, bf16[344,4096]{1,0:T(8,128)(2,1)} %bitcast.11, bf16[344,4096]{1,0:T(8,128)(2,1)} %wd_hbm.1, f32[1,4096]{1,0:T(1,128)} %bitcast.12, bf16[1000,4096]{1,0:T(8,128)(2,1)} %bitcast.9, ...), custom_call_target="tpu_custom_call" | custom-call | tf_op jit(solution)/shard_map/tail/pallas_call | solution.py:464
  156.7 0.6 fusion
  157.3 11.4 %layout.1 = bf16[512,32000]{1,0:T(8,128)(2,1)} custom-call(bf16[2,4,4,512,1024]{4,3,2,1,0:T(8,128)(2,1)S(1)} %get-tuple-element.7.g), custom_call_target="tpu_custom_call" | custom-call | tf_op jit(solution)/shard_map/layout/pallas_call | solution.py:488

commit v5 on v4

--- a/solution.py
+++ b/solution.py
@@ -14,6 +14,8 @@
 PIECE = 1024
 CHUNK = 128
 GROUP = 256
+BEFORE = 2
+SETTLE = 4
 LAG = 1
 
 def place(side):
@@ -116,13 +118,17 @@
         yield
         if b == 0:
             loads["wd"].wait()
-            pl.semaphore_wait(barrier, n_dev - 1)
         for p in range(pieces):
             Y[p, cut] = bf16(
                 jnp.dot(a, WD[:, p * PIECE:(p + 1) * PIECE], preferred_element_type=jnp.float32))
-            for q in range(b * GROUP // CHUNK, (b + 1) * GROUP // CHUNK):
-                theirs = Y.at[p, pl.ds(pl.multiple_of(q * CHUNK + (1 - c) * n1, n1), n1)]
-                start(remote(theirs, G.at[0, 1, p, pl.ds(q * CHUNK, n1)], (ssem, rsem), 26 * q + p, PT), q)
+            if b == 0 and p < BEFORE:
+                continue
+            if b == 0 and p == BEFORE:
+                pl.semaphore_wait(barrier, n_dev - 1)
+            for p2 in range(p + 1) if b == 0 and p == BEFORE else (p,):
+                for q in range(b * per, (b + 1) * per):
+                    theirs = Y.at[p2, pl.ds(pl.multiple_of(q * CHUNK + (1 - c) * n1, n1), n1)]
+                    start(remote(theirs, G.at[0, 1, p2, pl.ds(q * CHUNK, n1)], (ssem, rsem), 26 * q + p2, PT), q)
 
     def chain(b):
         sems = (ssem, rsem)
@@ -262,7 +268,7 @@
                 src_ref=ST.at[b, me], dst_ref=ST.at[b, me], send_sem=stsem.at[b, t], recv_sem=strsem.at[b, t],
                 device_id={"tp": to}, device_id_type=MESH).start()
             return 0
-        lax.fori_loop(0, n_dev - 1, body, 0)
+        lax.fori_loop(0, n_dev - 1, body, 0, unroll=True)
 
     def heard(b, wait):
         def body(t, _):
@@ -272,7 +278,7 @@
                 device_id={"tp": frm}, device_id_type=MESH)
             wait(cp)
             return 0
-        lax.fori_loop(0, n_dev - 1, body, 0)
+        lax.fori_loop(0, n_dev - 1, body, 0, unroll=True)
 
     sems = (gssem, grsem)
 
@@ -286,10 +292,10 @@
         return G.at[c, a, b, pl.ds(k * CHUNK, CHUNK)]
 
     def move(ref, k, q, to):
-        start(remote(ref, ref, sems, 22 * k + q, to))
+        start(remote(ref, ref, sems, 25 * k + q, to))
 
     def got(ref, k, q):
-        remote(ref, ref, sems, 22 * k + q, PT).wait_recv()
+        remote(ref, ref, sems, 25 * k + q, PT).wait_recv()
 
     def combine(b):
         group, part = b // per, b % per
@@ -323,44 +329,53 @@
         got(blk(right, k, 1), k, 1)
         move(blk(right, k, 1), k, 5, L1)
 
-    def second(k):
+    OWN, LEFT, RIGHT, FAR = range(4)
+    stand = (i, prv(i), nxt(i), opp(i))
+
+    def send(k, z, right=True, left=True):
+        b = one_of(stand[z], j, k)
+        if right:
+            move(b, k, 6 + z, R2)
+        if left:
+            move(b, k, 10 + z, L2)
+
+    def sides(k):
         got(blk(prv(i), k, 1), k, 2)
         got(blk(nxt(i), k, 0), k, 3)
+
+    def far_side(k):
         got(blk(opp(i), k, 0), k, 4)
         got(blk(opp(i), k, 1), k, 5)
+
+    def second(k):
+        far_side(k)
+        send(k, FAR)
         move(line(j, k), k, 18, PT)
 
-    toR = tuple(range(side))
-    toL = toR[side // 2:] + toR[:side // 2]
-
-    def send(k, q):
-        move(one_of(toR[q], j, k), k, 6 + q, R2)
-        move(one_of(toL[q], j, k), k, 6 + side + q, L2)
-
     def third(k):
-        for q in range(side // 2):
-            b = one_of(toR[q], prv(j), k)
-            got(b, k, 6 + q)
-            move(b, k, 6 + 2 * side + q, R2)
-            b = one_of(toL[q], nxt(j), k)
-            got(b, k, 6 + side + q)
-            move(b, k, 6 + 2 * side + side // 2 + q, L2)
+        for z, base, frm, sem, to in ((OWN, 6, prv(j), 14, R2), (LEFT, 10, nxt(j), 16, L2),
+                                      (RIGHT, 6, prv(j), 15, R2), (FAR, 10, nxt(j), 17, L2)):
+            b = one_of(stand[z], frm, k)
+            got(b, k, base + z)
+            move(b, k, sem, to)
 
     def fourth(k):
-        for q in range(side // 2, side):
-            got(one_of(toR[q], prv(j), k), k, 6 + q)
+        for z in (LEFT, FAR):
+            got(one_of(stand[z], prv(j), k), k, 6 + z)
         move(line(prv(j), k), k, 19, PT)
-        for q in range(side // 2, side):
-            got(one_of(toL[q], nxt(j), k), k, 6 + side + q)
+        for z in (OWN, RIGHT):
+            got(one_of(stand[z], nxt(j), k), k, 10 + z)
         move(line(nxt(j), k), k, 20, PT)
-        for q in range(side // 2):
-            got(one_of(toR[q], opp(j), k), k, 6 + 2 * side + q)
-            got(one_of(toL[q], opp(j), k), k, 6 + 2 * side + side // 2 + q)
-        move(line(opp(j), k), k, 21, PT)
+        for z, sem in ((OWN, 14), (LEFT, 16), (RIGHT, 15), (FAR, 17)):
+            b = one_of(stand[z], opp(j), k)
+            got(b, k, sem)
+            move(b, k, 21 + z, PT)
 
     def last(k):
-        for q, g in enumerate((i, prv(i), nxt(i), opp(i))):
+        for q, g in enumerate((i, prv(i), nxt(i))):
             got(G.at[1 - c, :, g, pl.ds(k * CHUNK, CHUNK)], k, 18 + q)
+        for z, a in enumerate((j, prv(j), nxt(j), opp(j))):
+            got(G.at[1 - c, a, opp(i), pl.ds(k * CHUNK, CHUNK)], k, 21 + z)
 
     def lockstep(g):
         mine = [chain(b) for b in range(g * per, (g + 1) * per)]
@@ -387,37 +402,47 @@
         if rnd > LAG:
             next(two)
     def both(k):
-        second(k)
-        for q in range(side):
-            send(k, q)
+        sides(k)
+        far_side(k)
+        for zr, zl in ((OWN, LEFT), (RIGHT, FAR), (LEFT, OWN), (FAR, RIGHT)):
+            send(k, zr, left=False)
+            send(k, zl, right=False)
+        move(line(j, k), k, 18, PT)
 
     logits(0)
     next(two)
     combine(0)
+    send(0, OWN)
     combine(1)
     next(two, None)
     first(0)
     next(two, None)
-    second(0)
-    send(0, 0)
+    sides(0)
+    send(0, LEFT)
+    next(two, None)
+    send(0, RIGHT)
     first(1)
-    next(two, None)
-    send(0, 1)
     for _ in two:
         pass
-    send(0, 2)
+    second(0)
     logits(1)
-    send(0, 3)
     third(0)
     both(1)
     combine(2)
     combine(3)
+    for b in range(groups):
+        heard(b, lambda cp: cp.wait_send())
+    marks = [0] * SETTLE
+    settled = 0
     for act, k in ((first, 2), (third, 1), (first, 3), (fourth, 0), (both, 2), (fourth, 1), (both, 3), (last, 0),
                    (third, 2), (last, 1), (third, 3), (fourth, 2), (last, 2), (fourth, 3), (last, 3)):
+        upto = marks[-SETTLE]
+        for cp in sent[settled:upto]:
+            cp.wait_send()
+        settled = max(settled, upto)
+        marks.append(len(sent))
         act(k)
-    for b in range(groups):
-        heard(b, lambda cp: cp.wait_send())
-    for cp in sent:
+    for cp in sent[settled:]:
         cp.wait_send()
 
 
@@ -476,7 +501,7 @@
                 pltpu.VMEM((groups, n_dev, 8, CHUNK), jnp.float32),
                 dma((3 * (d // PIECE) + groups + 1,)),
                 dma((26 * chunks,)), dma((26 * chunks,)),
-                dma((22 * chunks,)), dma((22 * chunks,)),
+                dma((25 * chunks,)), dma((25 * chunks,)),
                 dma((groups, n_dev - 1)), dma((groups, n_dev - 1)),
             ],
             compiler_params=pltpu.CompilerParams(

time: 169 us -> 167 us (0.988)
  no operation moved by 1% of the time
where the time goes in v5:
time: 167 us
  Pallas kernels  166 us (99%)
    pallas_call x1, Pallas kernels, device_step(): pl.pallas_call(functools.partial(tail_kernel, side, n_dev, f_loc, v_loc),...  154 us
    pallas_call x1, Pallas kernels, device_step(): pl.pallas_call(functools.partial(layout_kernel, side, v_loc), out_shape=j...  11.4 us

profile of v5, /device:TPU:97, one launch (start us, length us, event | category | flops | bytes accessed | tf_op | source)
XLA Modules:
  0.0 167.2 jit_solution(1544845850829215224)
XLA Ops:
  0.6 154.4 %tail.1 = (bf16[2,4,4,512,1024]{4,3,2,1,0:T(8,128)(2,1)S(1)}, f32[8,512]{1,0:T(8,128)S(1)}) custom-call(bf16[512,4096]{1,0:T(8,128)(2,1)} %h_hbm.1, bf16[344,4096]{1,0:T(8,128)(2,1)} %bitcast.10, bf16[344,4096]{1,0:T(8,128)(2,1)} %bitcast.11, bf16[344,4096]{1,0:T(8,128)(2,1)} %wd_hbm.1, f32[1,4096]{1,0:T(1,128)} %bitcast.12, bf16[1000,4096]{1,0:T(8,128)(2,1)} %bitcast.9, ...), custom_call_target="tpu_custom_call" | custom-call | tf_op jit(solution)/shard_map/tail/pallas_call | solution.py:489
  155.1 0.6 fusion
  155.7 11.4 %layout.1 = bf16[512,32000]{1,0:T(8,128)(2,1)} custom-call(bf16[2,4,4,512,1024]{4,3,2,1,0:T(8,128)(2,1)S(1)} %get-tuple-element.7.g), custom_call_target="tpu_custom_call" | custom-call | tf_op jit(solution)/shard_map/layout/pallas_call | solution.py:513

commit v6 on v5

--- a/solution.py
+++ b/solution.py
@@ -314,11 +314,9 @@
         out[1:2, cols] = ln - w / s
         out[2:3, cols] = t - ln
 
-        def turn(q, _):
-            v = pl.ds(pl.multiple_of(q * 128, 128), 128)
+        for v in range(0, vpad, 128):
+            v = slice(v, v + 128)
             G[c, i, j, cols, v] = bf16((LT[group, v, part * CHUNK:(part + 1) * CHUNK] - ln).T)
-            return 0
-        lax.fori_loop(0, vpad // 128, turn, 0)
         for q, (bit, to) in enumerate(((0, R1), (1, L1), (1, R1), (0, L1))):
             move(blk(i, b, bit), b, q, to)
 

time: 167 us -> 167 us (level)
  no operation moved by 1% of the time
where the time goes in v6:
time: 167 us
  Pallas kernels  165 us (99%)
    pallas_call x1, Pallas kernels, device_step(): pl.pallas_call(functools.partial(tail_kernel, side, n_dev, f_loc, v_loc),...  154 us
    pallas_call x1, Pallas kernels, device_step(): pl.pallas_call(functools.partial(layout_kernel, side, v_loc), out_shape=j...  11.4 us

profile of v6, /device:TPU:97, one launch (start us, length us, event | category | flops | bytes accessed | tf_op | source)
XLA Modules:
  0.0 166.5 jit_solution(10784074630276972524)
XLA Ops:
  0.6 153.7 %tail.1 = (bf16[2,4,4,512,1024]{4,3,2,1,0:T(8,128)(2,1)S(1)}, f32[8,512]{1,0:T(8,128)S(1)}) custom-call(bf16[512,4096]{1,0:T(8,128)(2,1)} %h_hbm.1, bf16[344,4096]{1,0:T(8,128)(2,1)} %bitcast.10, bf16[344,4096]{1,0:T(8,128)(2,1)} %bitcast.11, bf16[344,4096]{1,0:T(8,128)(2,1)} %wd_hbm.1, f32[1,4096]{1,0:T(1,128)} %bitcast.12, bf16[1000,4096]{1,0:T(8,128)(2,1)} %bitcast.9, ...), custom_call_target="tpu_custom_call" | custom-call | tf_op jit(solution)/shard_map/tail/pallas_call | solution.py:487
  154.4 0.6 fusion
  154.9 11.4 %layout.1 = bf16[512,32000]{1,0:T(8,128)(2,1)} custom-call(bf16[2,4,4,512,1024]{4,3,2,1,0:T(8,128)(2,1)S(1)} %get-tuple-element.7.g), custom_call_target="tpu_custom_call" | custom-call | tf_op jit(solution)/shard_map/layout/pallas_call | solution.py:511
